TPU v7x, 32 devices: a whole 2x2x4 slice. The times are simulated.
32 devices in a mesh: gx: 4 (over x, core), gy: 4 (over z), gz: 2 (over y).
Axes of the slice: x: 2, y: 2, z: 4, core: 2. Of those that a mesh axis runs over, the one named last changes fastest.
Arguments:
- orbitals: float32 [16, 48, 48, 256], P(None, 'gx', 'gy', 'gz'), may hold values from -6 to 6
- potential: float32 [48, 48, 256], P('gx', 'gy', 'gz'), may hold values from 0 to 2
Outputs:
- filtered: float32 [16, 48, 48, 256], P(None, 'gx', 'gy', 'gz')
All inputs are finite; a program needn't handle non-finite values.
Results may differ from a plain program's by a relative error of at most 0.00002.
Values sent between devices are 32-bit elements; how exact they have to be, the bound alone decides.
A program may use at most 64 MiB of HBM per device.

v0:
```python
import functools
import math

import jax
import jax.numpy as jnp
import numpy as np
from jax import lax
from jax.experimental import pallas as pl
from jax.experimental.pallas import tpu as pltpu
from jax.sharding import PartitionSpec as P

DEGREE = 2
SECOND = (
    -5369.0 / 1800.0,
    12.0 / 7.0,
    -15.0 / 56.0,
    10.0 / 189.0,
    -1.0 / 112.0,
    2.0 / 1925.0,
    -1.0 / 16632.0,
)
FIRST = (6.0 / 7.0, -15.0 / 56.0, 5.0 / 63.0, -1.0 / 56.0, 3.0 / 385.0, -1.0 / 792.0)
METRIC = ((1.0, 0.25, 0.15), (0.25, 1.0, 0.2), (0.15, 0.2, 1.0))
CENTER = 10.5
HALF_WIDTH = 9.5
R = 6
Y0 = 8
MESH = pl.DeviceIdType.MESH


def z_matrices(bz):
    w = np.zeros((bz + 128, 2 * bz), np.float64)

    def row(p):
        return p if 0 <= p < bz else (bz + 8 + p if p < 0 else p + 8)

    for n in range(bz):
        for k in range(1, R + 1):
            w[row(n + k), n] += FIRST[k - 1]
            w[row(n - k), n] -= FIRST[k - 1]
            w[row(n + k), bz + n] += -0.5 * METRIC[2][2] * SECOND[k]
            w[row(n - k), bz + n] += -0.5 * METRIC[2][2] * SECOND[k]
    high = w.astype(np.float32).astype(jnp.bfloat16)
    low = (w - high.astype(np.float64)).astype(np.float32).astype(jnp.bfloat16)
    return jnp.asarray(high), jnp.asarray(low)


def kernel(
    gx, gy, gz, bx, by,
    orb, pot, whi_ref, wlo_ref, out,
    vin, pin, p_ref, v0, v1, a_ref, c0, c1, s_ref, obuf, ebuf, hbuf,
    isend, irecv, psend, precv, qsend, qrecv, hsend, hrecv, osend, orecv, lsem,
):
    bz = orb.shape[-1]
    nx, ny = gx * bx, gy * by
    group = 8 // math.gcd(by, 8)
    rows = bx * ny
    padded_rows = ebuf.shape[-1]
    cx, cy, cz = lax.axis_index("gx"), lax.axis_index("gy"), lax.axis_index("gz")
    band = cx * gy + cy
    zl, zr = lax.rem(cz + gz - 1, gz), lax.rem(cz + 1, gz)
    far_first = sorted(range(1, gy), key=lambda d: -min(d, gy - d))

    barrier = pltpu.get_barrier_semaphore()
    for dx in range(gx):
        for dy in range(gy):
            if dx or dy:
                pl.semaphore_signal(
                    barrier, inc=1,
                    device_id=(lax.rem(cx + dx, gx), lax.rem(cy + dy, gy), cz),
                    device_id_type=MESH,
                )
    for z in (zl, zr):
        pl.semaphore_signal(barrier, inc=1, device_id=(cx, cy, z), device_id_type=MESH)
    pl.semaphore_wait(barrier, gx * gy + 1)

    own_pot = pltpu.make_async_copy(pot, pin.at[cx, cy], lsem.at[1])
    own_pot.start()
    gathers = [own_pot]
    for dy in far_first:
        copy = pltpu.make_async_remote_copy(
            pot, pin.at[cx, cy], psend.at[dy], precv.at[dy],
            device_id=(cx, lax.rem(cy + dy, gy), cz), device_id_type=MESH,
        )
        copy.start()
        gathers.append(copy)

    def send_bands(dx):
        tx = lax.rem(cx + dx, gx)
        copies = []
        for dy in far_first + [0]:
            ty = lax.rem(cy + dy, gy)
            n = dx * gy + dy
            if n == 0:
                copy = pltpu.make_async_copy(orb.at[band], vin.at[cx, cy], lsem.at[0])
            else:
                copy = pltpu.make_async_remote_copy(
                    orb.at[tx * gy + ty], vin.at[cx, cy], isend.at[n], irecv.at[n],
                    device_id=(tx, ty, cz), device_id_type=MESH,
                )
            copy.start()
            copies.append(copy)
        return copies

    spread_steps = []
    d = gx // 2
    while d:
        spread_steps.append(d)
        d //= 2
    held = [cx]
    spread_count = [0]

    def spread(d):
        bit = lax.rem(lax.div(cx, d), 2)
        hop = d - 2 * d * bit
        copies = []
        for r in list(held):
            i = spread_count[0]
            spread_count[0] += 1
            copy = pltpu.make_async_remote_copy(
                pin.at[r], pin.at[r], qsend.at[i], qrecv.at[i],
                device_id=(cx + hop, cy, cz), device_id_type=MESH,
            )
            copy.start()
            copies.append(copy)
            held.append(r + hop)
        return copies

    def wrap_y(ref, x):
        ref[x, pl.ds(Y0 - R, R), :] = ref[x, pl.ds(Y0 + ny - R, R), :]
        ref[x, pl.ds(Y0 + ny, R), :] = ref[x, pl.ds(Y0, R), :]

    def wrap_x(ref, sx):
        @pl.when(sx == 0)
        def _():
            ref[pl.ds(nx + R, R)] = ref[pl.ds(R, R)]

        @pl.when(sx == gx - 1)
        def _():
            ref[pl.ds(0, R)] = ref[pl.ds(nx, R)]

    def pieces(ref, sx, i):
        at = pl.multiple_of(i * group * by, 8)
        for sy in range(gy):
            got = ref[sx, sy, pl.ds(at, group * by), :]
            for j in range(group):
                yield sy, j, got[j * by : (j + 1) * by]

    def assemble(sx):
        @pl.loop(0, bx // group)
        def _(i):
            x = sx * bx + i * group + R
            for sy, j, piece in pieces(vin, sx, i):
                v0[x + j, pl.ds(Y0 + sy * by, by), :] = piece
            for j in range(group):
                wrap_y(v0, x + j)
        wrap_x(v0, sx)

    def assemble_potential():
        for sx in range(gx):
            @pl.loop(0, bx // group)
            def _(i):
                x = sx * bx + i * group
                for sy, j, piece in pieces(pin, sx, i):
                    p_ref[x + j, pl.ds(sy * by, by), :] = piece + (-1.5 * SECOND[0] - CENTER)

    def send_edges(step, v, sx, t):
        vals = v[pl.ds(sx * bx + R, bx), pl.ds(Y0, ny), :].reshape(rows, bz)
        if padded_rows > rows:
            vals = jnp.concatenate([vals, jnp.zeros((padded_rows - rows, bz), jnp.float32)], axis=0)
        for i in range(padded_rows // 128):
            turned = vals[i * 128 : (i + 1) * 128].T
            ebuf[step, t, 0, :, pl.ds(i * 128, 128)] = turned[:8]
            ebuf[step, t, 1, :, pl.ds(i * 128, 128)] = turned[bz - 8 :]
        copies = []
        for side, z in ((0, zl), (1, zr)):
            copy = pltpu.make_async_remote_copy(
                ebuf.at[step, t, side], hbuf.at[step, t, 1 - side],
                hsend.at[step, t, side], hrecv.at[step, t, 1 - side],
                device_id=(cx, cy, z), device_id_type=MESH,
            )
            copy.start()
            copies.append(copy)
        return copies

    def y_pass(v, c_ref, sx):
        @pl.loop(0, bx)
        def _(i):
            x = sx * bx + i
            first = second = None
            for k in range(1, R + 1):
                up = v[x + R, pl.ds(Y0 + k, ny), :]
                down = v[x + R, pl.ds(Y0 - k, ny), :]
                f = (-METRIC[0][1] * FIRST[k - 1]) * (up - down)
                s = (-0.5 * METRIC[1][1] * SECOND[k]) * (up + down)
                first = f if first is None else first + f
                second = s if second is None else second + s
            c_ref[x + R] = first
            s_ref[x] = second

    def z_pass(step, v, c_ref, sx, t):
        vals = v[pl.ds(sx * bx + R, bx), pl.ds(Y0, ny), :].reshape(rows, bz)
        sides = []
        for i in range(padded_rows // 128):
            block = jnp.concatenate(
                [
                    hbuf[step, t, 0, :, pl.ds(i * 128, 128)],
                    hbuf[step, t, 1, :, pl.ds(i * 128, 128)],
                    jnp.zeros((112, 128), jnp.float32),
                ],
                axis=0,
            )
            sides.append(block.T)
        full = jnp.concatenate([vals, jnp.concatenate(sides, axis=0)[:rows]], axis=1)
        high = full.astype(jnp.bfloat16)
        low = (full - high.astype(jnp.float32)).astype(jnp.bfloat16)
        dot = functools.partial(jnp.dot, preferred_element_type=jnp.float32)
        whi = whi_ref[...]
        got = dot(high, whi) + (dot(low, whi) + dot(high, wlo_ref[...]))
        a = got[:, :bz].reshape(bx, ny, bz)
        s_ref[pl.ds(sx * bx, bx)] += got[:, bz:].reshape(bx, ny, bz)
        c_ref[pl.ds(sx * bx + R, bx)] += (-METRIC[0][2]) * a
        a_ref[pl.ds(sx * bx, bx), pl.ds(Y0, ny), :] = a
        for i in range(bx):
            wrap_y(a_ref, sx * bx + i)
        wrap_x(c_ref, sx)

    def x_row(v, c_ref, x):
        total = s_ref[x] + p_ref[x] * v[x + R, pl.ds(Y0, ny), :]
        for k in range(1, R + 1):
            total = total + (-0.5 * METRIC[0][0] * SECOND[k]) * (
                v[x + R + k, pl.ds(Y0, ny), :] + v[x + R - k, pl.ds(Y0, ny), :]
            )
            total = total + FIRST[k - 1] * (c_ref[x + R + k] - c_ref[x + R - k])
            total = total + (-METRIC[1][2] * FIRST[k - 1]) * (
                a_ref[x, pl.ds(Y0 + k, ny), :] - a_ref[x, pl.ds(Y0 - k, ny), :]
            )
        return total

    def wait_all(copies):
        for copy in copies:
            copy.wait()

    block = [lax.rem(cx + gx - t, gx) for t in range(gx)]
    second_edges = {}

    def first_x_pass(t):
        sx = block[t]

        @pl.loop(0, bx)
        def _(i):
            x = sx * bx + i
            v1[x + R, pl.ds(Y0, ny), :] = (1.0 / HALF_WIDTH) * x_row(v0, c0, x)
            wrap_y(v1, x + R)
        wrap_x(v1, sx)
        second_edges[t] = send_edges(1, v1, sx, t)
        y_pass(v1, c1, sx)

    half = (gx + 1) // 2
    bands_in = [send_bands(dx) for dx in range(half)]
    wait_all(gathers)
    doing = spread(spread_steps[0])
    bands_in += [send_bands(dx) for dx in range(half, gx)]
    first_edges = []
    for t in range(gx):
        wait_all(bands_in[t])
        assemble(block[t])
        first_edges.append(send_edges(0, v0, block[t], t))
        y_pass(v0, c0, block[t])
        if 1 <= t < gx - 1:
            wait_all(doing)
            doing = spread(spread_steps[t]) if t < len(spread_steps) else []
        if t == gx - 1:
            wait_all(doing)
            assemble_potential()
        if t >= 1:
            wait_all(first_edges[t - 1])
            z_pass(0, v0, c0, block[t - 1], t - 1)
    for t in range(1, gx - 2):
        first_x_pass(t)
    wait_all(first_edges[gx - 1])
    z_pass(0, v0, c0, block[gx - 1], gx - 1)
    late = [gx - 2, gx - 1, 0]
    for t in late:
        first_x_pass(t)

    outgoing = []

    def last_x_pass(t):
        sx = block[t]

        @pl.loop(0, bx // group)
        def _(i):
            got = []
            for j in range(group):
                x = sx * bx + i * group + j
                got.append(
                    (2.0 / HALF_WIDTH) * x_row(v1, c1, x) - v0[x + R, pl.ds(Y0, ny), :]
                )
            at = pl.multiple_of(i * group * by, 8)
            for sy in range(gy):
                obuf[sx, sy, pl.ds(at, group * by), :] = jnp.concatenate(
                    [g[sy * by : (sy + 1) * by] for g in got], axis=0
                )

        for dy in far_first + [0]:
            ty = lax.rem(cy + dy, gy)
            n = t * gy + dy
            if n == 0:
                copy = pltpu.make_async_copy(obuf.at[sx, ty], out.at[band], lsem.at[2])
            else:
                copy = pltpu.make_async_remote_copy(
                    obuf.at[sx, ty], out.at[band], osend.at[n], orecv.at[n],
                    device_id=(sx, ty, cz), device_id_type=MESH,
                )
            copy.start()
            outgoing.append(copy)

    ready = list(range(1, gx - 2)) + late
    done = []
    for t in ready:
        wait_all(second_edges[t])
        z_pass(1, v1, c1, block[t], t)
        done.append(t)
        for u in range(gx):
            near = {u, (u + 1) % gx, (u - 1) % gx}
            if near <= set(done) and t in near:
                last_x_pass(u)
    wait_all(outgoing)


def local(sizes, orbitals, potential):
    gx, gy, gz = sizes
    bands, bx, by, bz = orbitals.shape
    nx, ny = gx * bx, gy * by
    assert bands == gx * gy and gz > 1 and gx >= 4 and gx & (gx - 1) == 0
    f32 = jnp.float32
    whi, wlo = z_matrices(bz)
    anywhere = pl.BlockSpec(memory_space=pl.ANY)
    vmem = pl.BlockSpec(memory_space=pltpu.VMEM)
    dma = pltpu.SemaphoreType.DMA
    edge = (DEGREE, gx, 2, 8, (bx * ny + 127) // 128 * 128)
    out = pl.pallas_call(
        functools.partial(kernel, gx, gy, gz, bx, by),
        out_shape=jax.ShapeDtypeStruct((bands, bx * by, bz), f32),
        in_specs=[anywhere, anywhere, vmem, vmem],
        out_specs=anywhere,
        scratch_shapes=[
            pltpu.VMEM((gx, gy, bx * by, bz), f32),
            pltpu.VMEM((gx, gy, bx * by, bz), f32),
            pltpu.VMEM((nx, ny, bz), f32),
            pltpu.VMEM((nx + 2 * R, ny + 16, bz), f32),
            pltpu.VMEM((nx + 2 * R, ny + 16, bz), f32),
            pltpu.VMEM((nx, ny + 16, bz), f32),
            pltpu.VMEM((nx + 2 * R, ny, bz), f32),
            pltpu.VMEM((nx + 2 * R, ny, bz), f32),
            pltpu.VMEM((nx, ny, bz), f32),
            pltpu.VMEM((gx, gy, bx * by, bz), f32),
            pltpu.VMEM(edge, f32),
            pltpu.VMEM(edge, f32),
            dma((gx * gy,)), dma((gx * gy,)),
            dma((gy,)), dma((gy,)),
            dma((gx,)), dma((gx,)),
            dma((DEGREE, gx, 2)), dma((DEGREE, gx, 2)),
            dma((gx * gy,)), dma((gx * gy,)),
            dma((3,)),
        ],
        compiler_params=pltpu.CompilerParams(
            collective_id=0, has_side_effects=True, vmem_limit_bytes=48 * 1024 * 1024
        ),
    )(
        orbitals.reshape(bands, bx * by, bz),
        potential.reshape(bx * by, bz),
        whi,
        wlo,
    )
    return out.reshape(bands, bx, by, bz)


def solution(mesh):
    sizes = tuple(mesh.shape[a] for a in ("gx", "gy", "gz"))
    return jax.shard_map(
        functools.partial(local, sizes),
        mesh=mesh,
        in_specs=(P(None, "gx", "gy", "gz"), P("gx", "gy", "gz")),
        out_specs=P(None, "gx", "gy", "gz"),
        check_vma=False,
    )
```

profile of v0, /device:TPU:0, one launch (start us, length us, event | category | flops | bytes accessed | tf_op | source)
XLA Modules:
  0.0 81.1 jit_solution(7601480268721228090)
XLA Ops:
  0.0 0.9 %reshape.10.pot = f32[144,128]{1,0:T(8,128)S(1)} reshape(f32[12,12,128]{2,1,0:T(8,128)} %param.5) | data formatting | bytes 147456 | tf_op jit(solution)/shard_map/reshape | solution.py:373
  0.9 0.0 copy-start
  0.9 0.0 copy-start.1
  0.9 1.7 %copy.7.orb = f32[16,144,128]{2,1,0:T(8,128)S(1)} copy(f32[16,144,128]{2,0,1:T(8,128)} %bitcast.2) | data formatting | bytes 2359296 | tf_op jit(solution)/shard_map/reshape | solution.py:372
  2.6 0.0 copy-done
  2.6 0.0 copy-done.1
  2.6 77.1 %shard_map.46 = f32[16,144,128]{2,1,0:T(8,128)S(1)} custom-call(f32[16,144,128]{2,1,0:T(8,128)S(1)} %copy.7.orb, f32[144,128]{1,0:T(8,128)S(1)} %reshape.10.pot, bf16[256,256]{1,0:T(8,128)(2,1)S(1)} %copy-done.1, bf16[256,256]{1,0:T(8,128)(2,1)S(1)} %copy-done), custom_call_target="tpu_custom_call" | custom-call | tf_op jit(solution)/shard_map/pallas_call | solution.py:343
  79.8 1.4 %copy.8 = f32[16,144,128]{2,0,1:T(8,128)} copy(f32[16,144,128]{2,1,0:T(8,128)S(1)} %shard_map.46) | data formatting | bytes 2359296 | tf_op jit(solution)/shard_map/pallas_call | solution.py:343
Async XLA Ops:
  0.9 1.7 %copy-start = (bf16[256,256]{1,0:T(8,128)(2,1)S(1)}, bf16[256,256]{1,0:T(8,128)(2,1)}, u32[]{:S(2)}) copy-start(bf16[256,256]{1,0:T(8,128)(2,1)} %constant.5.clone.wlo_ref) | copy-start | bytes 393220
  0.9 1.7 %copy-start.1 = (bf16[256,256]{1,0:T(8,128)(2,1)S(1)}, bf16[256,256]{1,0:T(8,128)(2,1)}, u32[]{:S(2)}) copy-start(bf16[256,256]{1,0:T(8,128)(2,1)} %constant.4.clone.whi_ref) | copy-start | bytes 393220
where the time goes:
time: 81.3 us; the launch traced here: 81.1 us
  Pallas kernels  77.1 us (95%)
  local copies, waits for them, and re-layouts  3.98 us (5%)
    pallas_call x1, Pallas kernels, local(): pl.pallas_call(functools.partial(kernel, gx, gy, gz, bx, by), out_shape=j...  77.1 us
    reshape x1, local copies, waits for them, and re-layouts, local(): orbitals.reshape(bands, bx * by, bz)  1.7 us

commit v1 on v0

--- a/solution.py
+++ b/solution.py
@@ -59,7 +59,19 @@
     cx, cy, cz = lax.axis_index("gx"), lax.axis_index("gy"), lax.axis_index("gz")
     band = cx * gy + cy
     zl, zr = lax.rem(cz + gz - 1, gz), lax.rem(cz + 1, gz)
-    far_first = sorted(range(1, gy), key=lambda d: -min(d, gy - d))
+    odd = lax.rem(cx, 2)
+    chip = cx - odd
+    partner = chip + 1 - odd
+
+    def across(d):
+        ty, bit = cy, 1
+        while bit <= d:
+            if d & bit:
+                ty = ty + bit - 2 * bit * lax.rem(lax.div(cy, bit), 2)
+            bit *= 2
+        return ty
+
+    far_first = list(range(gy - 1, 0, -1))
 
     barrier = pltpu.get_barrier_semaphore()
     for dx in range(gx):
@@ -80,27 +92,39 @@
     for dy in far_first:
         copy = pltpu.make_async_remote_copy(
             pot, pin.at[cx, cy], psend.at[dy], precv.at[dy],
-            device_id=(cx, lax.rem(cy + dy, gy), cz), device_id_type=MESH,
+            device_id=(cx, across(dy), cz), device_id_type=MESH,
         )
         copy.start()
         gathers.append(copy)
 
-    def send_bands(dx):
-        tx = lax.rem(cx + dx, gx)
-        copies = []
-        for dy in far_first + [0]:
-            ty = lax.rem(cy + dy, gy)
-            n = dx * gy + dy
-            if n == 0:
-                copy = pltpu.make_async_copy(orb.at[band], vin.at[cx, cy], lsem.at[0])
+    own_band = pltpu.make_async_copy(orb.at[band], vin.at[cx, cy], lsem.at[0])
+    bands_out = []
+
+    def send_band(n, tx, ty):
+        copy = pltpu.make_async_remote_copy(
+            orb.at[tx * gy + ty], vin.at[cx, cy], isend.at[n], irecv.at[cx, cy],
+            device_id=(tx, ty, cz), device_id_type=MESH,
+        )
+        copy.start()
+        bands_out.append(copy)
+
+    def send_group(g):
+        for d in far_first + [0]:
+            for i in range(gx // 2):
+                if i or d:
+                    n = (g * (gx // 2) + i) * gy + d
+                    send_band(n, lax.rem(chip + 2 * i + g, gx), across(d))
+
+    def wait_block(sx, own):
+        for d in range(gy):
+            sy = across(d)
+            if own and d == 0:
+                own_band.wait()
             else:
-                copy = pltpu.make_async_remote_copy(
-                    orb.at[tx * gy + ty], vin.at[cx, cy], isend.at[n], irecv.at[n],
-                    device_id=(tx, ty, cz), device_id_type=MESH,
-                )
-            copy.start()
-            copies.append(copy)
-        return copies
+                pltpu.make_async_remote_copy(
+                    orb.at[band], vin.at[sx, sy], isend.at[0], irecv.at[sx, sy],
+                    device_id=(partner, cy, cz), device_id_type=MESH,
+                ).wait_recv()
 
     spread_steps = []
     d = gx // 2
@@ -241,7 +265,7 @@
         for copy in copies:
             copy.wait()
 
-    block = [lax.rem(cx + gx - t, gx) for t in range(gx)]
+    block = [lax.rem(cx + gx + t - 2 * t * odd, gx) for t in range(gx)]
     second_edges = {}
 
     def first_x_pass(t):
@@ -256,14 +280,15 @@
         second_edges[t] = send_edges(1, v1, sx, t)
         y_pass(v1, c1, sx)
 
-    half = (gx + 1) // 2
-    bands_in = [send_bands(dx) for dx in range(half)]
+    own_band.start()
+    send_band(0, partner, cy)
+    send_group(0)
     wait_all(gathers)
     doing = spread(spread_steps[0])
-    bands_in += [send_bands(dx) for dx in range(half, gx)]
+    send_group(1)
     first_edges = []
     for t in range(gx):
-        wait_all(bands_in[t])
+        wait_block(block[t], t == 0)
         assemble(block[t])
         first_edges.append(send_edges(0, v0, block[t], t))
         y_pass(v0, c0, block[t])
@@ -304,7 +329,7 @@
                 )
 
         for dy in far_first + [0]:
-            ty = lax.rem(cy + dy, gy)
+            ty = across(dy)
             n = t * gy + dy
             if n == 0:
                 copy = pltpu.make_async_copy(obuf.at[sx, ty], out.at[band], lsem.at[2])
@@ -327,6 +352,8 @@
             if near <= set(done) and t in near:
                 last_x_pass(u)
     wait_all(outgoing)
+    for copy in bands_out:
+        copy.wait_send()
 
 
 def local(sizes, orbitals, potential):
@@ -358,7 +385,7 @@
             pltpu.VMEM((gx, gy, bx * by, bz), f32),
             pltpu.VMEM(edge, f32),
             pltpu.VMEM(edge, f32),
-            dma((gx * gy,)), dma((gx * gy,)),
+            dma((gx * gy,)), dma((gx, gy)),
             dma((gy,)), dma((gy,)),
             dma((gx,)), dma((gx,)),
             dma((DEGREE, gx, 2)), dma((DEGREE, gx, 2)),

time: 81.3 us -> 82.6 us (1.016)
  Pallas kernels: 77.1 us -> 78.5 us
    pallas_call x1, Pallas kernels: 77.1 us -> 78.5 us  [local(): pl.pallas_call(functools.partial(kernel, gx, gy, gz, bx, by), out_shape=j...]
where the time goes in v1:
time: 82.6 us; the launch traced here: 82.5 us
  Pallas kernels  78.5 us (95%)
  local copies, waits for them, and re-layouts  3.98 us (5%)
    pallas_call x1, Pallas kernels, local(): pl.pallas_call(functools.partial(kernel, gx, gy, gz, bx, by), out_shape=j...  78.5 us
    reshape x1, local copies, waits for them, and re-layouts, local(): orbitals.reshape(bands, bx * by, bz)  1.7 us

profile of v1, /device:TPU:0, one launch (start us, length us, event | category | flops | bytes accessed | tf_op | source)
XLA Modules:
  0.0 82.5 jit_solution(17899655336122436710)
XLA Ops:
  0.0 0.9 %reshape.10.pot = f32[144,128]{1,0:T(8,128)S(1)} reshape(f32[12,12,128]{2,1,0:T(8,128)} %param.5) | data formatting | bytes 147456 | tf_op jit(solution)/shard_map/reshape | solution.py:400
  0.9 0.0 copy-start
  0.9 0.0 copy-start.1
  0.9 1.7 %copy.7.orb = f32[16,144,128]{2,1,0:T(8,128)S(1)} copy(f32[16,144,128]{2,0,1:T(8,128)} %bitcast.2) | data formatting | bytes 2359296 | tf_op jit(solution)/shard_map/reshape | solution.py:399
  2.6 0.0 copy-done
  2.6 0.0 copy-done.1
  2.6 78.5 %shard_map.46 = f32[16,144,128]{2,1,0:T(8,128)S(1)} custom-call(f32[16,144,128]{2,1,0:T(8,128)S(1)} %copy.7.orb, f32[144,128]{1,0:T(8,128)S(1)} %reshape.10.pot, bf16[256,256]{1,0:T(8,128)(2,1)S(1)} %copy-done.1, bf16[256,256]{1,0:T(8,128)(2,1)S(1)} %copy-done), custom_call_target="tpu_custom_call" | custom-call | tf_op jit(solution)/shard_map/pallas_call | solution.py:370
  81.1 1.4 %copy.8 = f32[16,144,128]{2,0,1:T(8,128)} copy(f32[16,144,128]{2,1,0:T(8,128)S(1)} %shard_map.46) | data formatting | bytes 2359296 | tf_op jit(solution)/shard_map/pallas_call | solution.py:370
Async XLA Ops:
  0.9 1.7 %copy-start = (bf16[256,256]{1,0:T(8,128)(2,1)S(1)}, bf16[256,256]{1,0:T(8,128)(2,1)}, u32[]{:S(2)}) copy-start(bf16[256,256]{1,0:T(8,128)(2,1)} %constant.5.clone.wlo_ref) | copy-start | bytes 393220
  0.9 1.7 %copy-start.1 = (bf16[256,256]{1,0:T(8,128)(2,1)S(1)}, bf16[256,256]{1,0:T(8,128)(2,1)}, u32[]{:S(2)}) copy-start(bf16[256,256]{1,0:T(8,128)(2,1)} %constant.4.clone.whi_ref) | copy-start | bytes 393220

commit v2 on v1

--- a/solution.py
+++ b/solution.py
@@ -87,15 +87,38 @@
     pl.semaphore_wait(barrier, gx * gy + 1)
 
     own_pot = pltpu.make_async_copy(pot, pin.at[cx, cy], lsem.at[1])
-    own_pot.start()
-    gathers = [own_pot]
-    for dy in far_first:
+    masks = []
+    m = gy - 1
+    while m:
+        masks.append(m)
+        m //= 2
+    mates = [lax.rem(cx + 2 * i, gx) for i in range(1, gx // 2)]
+    pot_out = []
+
+    def send_pot(src, x, y, target):
         copy = pltpu.make_async_remote_copy(
-            pot, pin.at[cx, cy], psend.at[dy], precv.at[dy],
-            device_id=(cx, across(dy), cz), device_id_type=MESH,
+            src, pin.at[x, y], psend.at[len(pot_out)], precv.at[x, y],
+            device_id=target + (cz,), device_id_type=MESH,
         )
         copy.start()
-        gathers.append(copy)
+        pot_out.append(copy)
+
+    def wait_pot(x, y):
+        pltpu.make_async_remote_copy(
+            pot, pin.at[x, y], psend.at[0], precv.at[x, y],
+            device_id=(partner, cy, cz), device_id_type=MESH,
+        ).wait_recv()
+
+    def share_pot():
+        copies = []
+        for i, x in enumerate([cx] + mates):
+            copy = pltpu.make_async_remote_copy(
+                pin.at[x], pin.at[x], qsend.at[i], qrecv.at[i],
+                device_id=(partner, cy, cz), device_id_type=MESH,
+            )
+            copy.start()
+            copies.append(copy)
+        return copies
 
     own_band = pltpu.make_async_copy(orb.at[band], vin.at[cx, cy], lsem.at[0])
     bands_out = []
@@ -108,9 +131,9 @@
         copy.start()
         bands_out.append(copy)
 
-    def send_group(g):
-        for d in far_first + [0]:
-            for i in range(gx // 2):
+    def send_group(g, pairs, ds):
+        for d in ds:
+            for i in pairs:
                 if i or d:
                     n = (g * (gx // 2) + i) * gy + d
                     send_band(n, lax.rem(chip + 2 * i + g, gx), across(d))
@@ -125,30 +148,6 @@
                     orb.at[band], vin.at[sx, sy], isend.at[0], irecv.at[sx, sy],
                     device_id=(partner, cy, cz), device_id_type=MESH,
                 ).wait_recv()
-
-    spread_steps = []
-    d = gx // 2
-    while d:
-        spread_steps.append(d)
-        d //= 2
-    held = [cx]
-    spread_count = [0]
-
-    def spread(d):
-        bit = lax.rem(lax.div(cx, d), 2)
-        hop = d - 2 * d * bit
-        copies = []
-        for r in list(held):
-            i = spread_count[0]
-            spread_count[0] += 1
-            copy = pltpu.make_async_remote_copy(
-                pin.at[r], pin.at[r], qsend.at[i], qrecv.at[i],
-                device_id=(cx + hop, cy, cz), device_id_type=MESH,
-            )
-            copy.start()
-            copies.append(copy)
-            held.append(r + hop)
-        return copies
 
     def wrap_y(ref, x):
         ref[x, pl.ds(Y0 - R, R), :] = ref[x, pl.ds(Y0 + ny - R, R), :]
@@ -280,23 +279,70 @@
         second_edges[t] = send_edges(1, v1, sx, t)
         y_pass(v1, c1, sx)
 
+    far = list(range(gy - 1, gy // 2 - 1, -1))
+    near = list(range(gy // 2 - 1, -1, -1))
+    others = list(range(1, gx // 2))
+
+    own_pot.start()
+    for d in masks:
+        send_pot(pot, cx, cy, (cx, across(d)))
+    for x in mates:
+        send_pot(pot, cx, cy, (x, cy))
     own_band.start()
     send_band(0, partner, cy)
-    send_group(0)
-    wait_all(gathers)
-    doing = spread(spread_steps[0])
-    send_group(1)
+    send_group(0, [0], far)
+    reached = [0]
+    for d in masks:
+        wait_pot(cx, across(d))
+    for x in mates:
+        wait_pot(x, cy)
+        for d in masks:
+            send_pot(pin.at[cx, across(d)], cx, across(d), (x, cy))
+    hops = []
+    for k, m in enumerate(masks):
+        if k:
+            hops.append((m, [o for o in reached if o]))
+        reached = reached + [o ^ m for o in reached]
+
+    def forward(x, hop):
+        m, offsets = hop
+        for o in offsets:
+            send_pot(pin.at[x, across(o)], x, across(o), (cx, across(m)))
+
+    def arrive(x, hop):
+        m, offsets = hop
+        for o in offsets:
+            wait_pot(x, across(o ^ m))
+
+    for hop in hops[:1]:
+        forward(cx, hop)
+    send_group(0, others, far + near)
+    for k, hop in enumerate(hops):
+        if k:
+            forward(cx, hop)
+        arrive(cx, hop)
+    for x in mates:
+        for d in masks:
+            wait_pot(x, across(d))
+        for hop in hops[:1]:
+            forward(x, hop)
+    send_group(0, [0], near)
+    for k, hop in enumerate(hops):
+        for x in mates:
+            if k:
+                forward(x, hop)
+            arrive(x, hop)
+    own_pot.wait()
+    sharing = share_pot()
+    send_group(1, [0] + others, near + far)
     first_edges = []
     for t in range(gx):
         wait_block(block[t], t == 0)
         assemble(block[t])
         first_edges.append(send_edges(0, v0, block[t], t))
         y_pass(v0, c0, block[t])
-        if 1 <= t < gx - 1:
-            wait_all(doing)
-            doing = spread(spread_steps[t]) if t < len(spread_steps) else []
         if t == gx - 1:
-            wait_all(doing)
+            wait_all(sharing)
             assemble_potential()
         if t >= 1:
             wait_all(first_edges[t - 1])
@@ -352,7 +398,7 @@
             if near <= set(done) and t in near:
                 last_x_pass(u)
     wait_all(outgoing)
-    for copy in bands_out:
+    for copy in bands_out + pot_out:
         copy.wait_send()
 
 
@@ -386,7 +432,7 @@
             pltpu.VMEM(edge, f32),
             pltpu.VMEM(edge, f32),
             dma((gx * gy,)), dma((gx, gy)),
-            dma((gy,)), dma((gy,)),
+            dma((2 * gx * gy,)), dma((gx, gy)),
             dma((gx,)), dma((gx,)),
             dma((DEGREE, gx, 2)), dma((DEGREE, gx, 2)),
             dma((gx * gy,)), dma((gx * gy,)),

time: 82.6 us -> 74.7 us (0.904)
  Pallas kernels: 78.5 us -> 70.5 us
    pallas_call x1, Pallas kernels: 78.5 us -> 70.5 us  [local(): pl.pallas_call(functools.partial(kernel, gx, gy, gz, bx, by), out_shape=j...]
where the time goes in v2:
time: 74.7 us; the launch traced here: 74.5 us
  Pallas kernels  70.5 us (94%)
  local copies, waits for them, and re-layouts  3.98 us (5%)
    pallas_call x1, Pallas kernels, local(): pl.pallas_call(functools.partial(kernel, gx, gy, gz, bx, by), out_shape=j...  70.5 us
    reshape x1, local copies, waits for them, and re-layouts, local(): orbitals.reshape(bands, bx * by, bz)  1.7 us

profile of v2, /device:TPU:0, one launch (start us, length us, event | category | flops | bytes accessed | tf_op | source)
XLA Modules:
  0.0 74.5 jit_solution(14367604238145110935)
XLA Ops:
  0.0 0.9 %reshape.10.pot = f32[144,128]{1,0:T(8,128)S(1)} reshape(f32[12,12,128]{2,1,0:T(8,128)} %param.5) | data formatting | bytes 147456 | tf_op jit(solution)/shard_map/reshape | solution.py:446
  0.9 0.0 copy-start
  0.9 0.0 copy-start.1
  0.9 1.7 %copy.7.orb = f32[16,144,128]{2,1,0:T(8,128)S(1)} copy(f32[16,144,128]{2,0,1:T(8,128)} %bitcast.2) | data formatting | bytes 2359296 | tf_op jit(solution)/shard_map/reshape | solution.py:445
  2.6 0.0 copy-done
  2.6 0.0 copy-done.1
  2.6 70.5 %shard_map.46 = f32[16,144,128]{2,1,0:T(8,128)S(1)} custom-call(f32[16,144,128]{2,1,0:T(8,128)S(1)} %copy.7.orb, f32[144,128]{1,0:T(8,128)S(1)} %reshape.10.pot, bf16[256,256]{1,0:T(8,128)(2,1)S(1)} %copy-done.1, bf16[256,256]{1,0:T(8,128)(2,1)S(1)} %copy-done), custom_call_target="tpu_custom_call" | custom-call | tf_op jit(solution)/shard_map/pallas_call | solution.py:416
  73.2 1.4 %copy.8 = f32[16,144,128]{2,0,1:T(8,128)} copy(f32[16,144,128]{2,1,0:T(8,128)S(1)} %shard_map.46) | data formatting | bytes 2359296 | tf_op jit(solution)/shard_map/pallas_call | solution.py:416
Async XLA Ops:
  0.9 1.7 %copy-start = (bf16[256,256]{1,0:T(8,128)(2,1)S(1)}, bf16[256,256]{1,0:T(8,128)(2,1)}, u32[]{:S(2)}) copy-start(bf16[256,256]{1,0:T(8,128)(2,1)} %constant.5.clone.wlo_ref) | copy-start | bytes 393220
  0.9 1.7 %copy-start.1 = (bf16[256,256]{1,0:T(8,128)(2,1)S(1)}, bf16[256,256]{1,0:T(8,128)(2,1)}, u32[]{:S(2)}) copy-start(bf16[256,256]{1,0:T(8,128)(2,1)} %constant.4.clone.whi_ref) | copy-start | bytes 393220

commit v3 on v2

--- a/solution.py
+++ b/solution.py
@@ -10,6 +10,7 @@
 from jax.sharding import PartitionSpec as P
 
 DEGREE = 2
+VMEM_BYTES = 54_300_000
 SECOND = (
     -5369.0 / 1800.0,
     12.0 / 7.0,
@@ -28,27 +29,45 @@
 MESH = pl.DeviceIdType.MESH
 
 
-def z_matrices(bz):
-    w = np.zeros((bz + 128, 2 * bz), np.float64)
-
-    def row(p):
-        return p if 0 <= p < bz else (bz + 8 + p if p < 0 else p + 8)
-
-    for n in range(bz):
+def halves(x):
+    high = float(np.float32(x).astype(jnp.bfloat16))
+    return high, float(np.float32(x - high).astype(jnp.bfloat16))
+
+
+def bands_of(offset, part):
+    out = []
+    for table, sign in ((FIRST, -1.0), ([-0.5 * METRIC[2][2] * c for c in SECOND[1:]], 1.0)):
+        acc = jnp.zeros(offset.shape, jnp.float32)
         for k in range(1, R + 1):
-            w[row(n + k), n] += FIRST[k - 1]
-            w[row(n - k), n] -= FIRST[k - 1]
-            w[row(n + k), bz + n] += -0.5 * METRIC[2][2] * SECOND[k]
-            w[row(n - k), bz + n] += -0.5 * METRIC[2][2] * SECOND[k]
-    high = w.astype(np.float32).astype(jnp.bfloat16)
-    low = (w - high.astype(np.float64)).astype(np.float32).astype(jnp.bfloat16)
-    return jnp.asarray(high), jnp.asarray(low)
+            value = halves(table[k - 1])[part]
+            acc = jnp.where(offset == k, value, acc)
+            acc = jnp.where(offset == -k, sign * value, acc)
+        out.append(acc)
+    return jnp.concatenate(out, axis=1).astype(jnp.bfloat16)
+
+
+def z_matrices(bz, inner_ref, outer_ref):
+    def index(shape, dim):
+        return lax.broadcasted_iota(jnp.int32, shape, dim)
+
+    square, edge = (bz, bz), (16, bz)
+    offset = index(square, 0) - index(square, 1)
+    e = index(edge, 0)
+    beyond = jnp.where(e < 8, e - 8, e - 8 + bz) - index(edge, 1)
+    high, edge_high = bands_of(offset, 0), bands_of(beyond, 0)
+    inner_ref[pl.ds(0, bz), :] = high
+    inner_ref[pl.ds(bz, bz), :] = high
+    outer_ref[pl.ds(0, bz), :] = bands_of(offset, 1)
+    outer_ref[pl.ds(bz, 16), :] = edge_high
+    outer_ref[pl.ds(bz + 16, 16), :] = edge_high
+    outer_ref[pl.ds(bz + 32, 16), :] = bands_of(beyond, 1)
+    outer_ref[pl.ds(bz + 48, 80), :] = jnp.zeros((80, 2 * bz), jnp.bfloat16)
 
 
 def kernel(
     gx, gy, gz, bx, by,
-    orb, pot, whi_ref, wlo_ref, out,
-    vin, pin, p_ref, v0, v1, a_ref, c0, c1, s_ref, obuf, ebuf, hbuf,
+    orb, pot, out,
+    inner_ref, outer_ref, vin, pin, p_ref, v0, v1, a_ref, c0, c1, s_ref, obuf, ebuf, hbuf,
     isend, irecv, psend, precv, qsend, qrecv, hsend, hrecv, osend, orecv, lsem,
 ):
     bz = orb.shape[-1]
@@ -73,6 +92,10 @@
 
     far_first = list(range(gy - 1, 0, -1))
 
+    own_pot = pltpu.make_async_copy(pot, pin.at[cx, cy], lsem.at[1])
+    own_pot.start()
+    own_band = pltpu.make_async_copy(orb.at[:, band], vin.at[cx, cy], lsem.at[0])
+    own_band.start()
     barrier = pltpu.get_barrier_semaphore()
     for dx in range(gx):
         for dy in range(gy):
@@ -86,7 +109,6 @@
         pl.semaphore_signal(barrier, inc=1, device_id=(cx, cy, z), device_id_type=MESH)
     pl.semaphore_wait(barrier, gx * gy + 1)
 
-    own_pot = pltpu.make_async_copy(pot, pin.at[cx, cy], lsem.at[1])
     masks = []
     m = gy - 1
     while m:
@@ -120,12 +142,11 @@
             copies.append(copy)
         return copies
 
-    own_band = pltpu.make_async_copy(orb.at[band], vin.at[cx, cy], lsem.at[0])
     bands_out = []
 
     def send_band(n, tx, ty):
         copy = pltpu.make_async_remote_copy(
-            orb.at[tx * gy + ty], vin.at[cx, cy], isend.at[n], irecv.at[cx, cy],
+            orb.at[:, tx * gy + ty], vin.at[cx, cy], isend.at[n], irecv.at[cx, cy],
             device_id=(tx, ty, cz), device_id_type=MESH,
         )
         copy.start()
@@ -145,7 +166,7 @@
                 own_band.wait()
             else:
                 pltpu.make_async_remote_copy(
-                    orb.at[band], vin.at[sx, sy], isend.at[0], irecv.at[sx, sy],
+                    orb.at[:, band], vin.at[sx, sy], isend.at[0], irecv.at[sx, sy],
                     device_id=(partner, cy, cz), device_id_type=MESH,
                 ).wait_recv()
 
@@ -162,10 +183,10 @@
         def _():
             ref[pl.ds(0, R)] = ref[pl.ds(nx, R)]
 
-    def pieces(ref, sx, i):
+    def pieces(sx, i):
         at = pl.multiple_of(i * group * by, 8)
         for sy in range(gy):
-            got = ref[sx, sy, pl.ds(at, group * by), :]
+            got = vin[sx, sy, pl.ds(at, group * by), :]
             for j in range(group):
                 yield sy, j, got[j * by : (j + 1) * by]
 
@@ -173,7 +194,7 @@
         @pl.loop(0, bx // group)
         def _(i):
             x = sx * bx + i * group + R
-            for sy, j, piece in pieces(vin, sx, i):
+            for sy, j, piece in pieces(sx, i):
                 v0[x + j, pl.ds(Y0 + sy * by, by), :] = piece
             for j in range(group):
                 wrap_y(v0, x + j)
@@ -181,11 +202,12 @@
 
     def assemble_potential():
         for sx in range(gx):
-            @pl.loop(0, bx // group)
+            @pl.loop(0, bx)
             def _(i):
-                x = sx * bx + i * group
-                for sy, j, piece in pieces(pin, sx, i):
-                    p_ref[x + j, pl.ds(sy * by, by), :] = piece + (-1.5 * SECOND[0] - CENTER)
+                for sy in range(gy):
+                    p_ref[sx * bx + i, pl.ds(sy * by, by), :] = pin[sx, sy, i] + (
+                        -1.5 * SECOND[0] - CENTER
+                    )
 
     def send_edges(step, v, sx, t):
         vals = v[pl.ds(sx * bx + R, bx), pl.ds(Y0, ny), :].reshape(rows, bz)
@@ -221,25 +243,25 @@
             c_ref[x + R] = first
             s_ref[x] = second
 
+    def split(x):
+        high = x.astype(jnp.bfloat16)
+        return high, (x - high.astype(jnp.float32)).astype(jnp.bfloat16)
+
     def z_pass(step, v, c_ref, sx, t):
         vals = v[pl.ds(sx * bx + R, bx), pl.ds(Y0, ny), :].reshape(rows, bz)
+        high, low = split(vals)
         sides = []
         for i in range(padded_rows // 128):
-            block = jnp.concatenate(
-                [
-                    hbuf[step, t, 0, :, pl.ds(i * 128, 128)],
-                    hbuf[step, t, 1, :, pl.ds(i * 128, 128)],
-                    jnp.zeros((112, 128), jnp.float32),
-                ],
-                axis=0,
+            edge = jnp.concatenate(
+                [hbuf[step, t, side, :, pl.ds(i * 128, 128)] for side in (0, 1)], axis=0
             )
-            sides.append(block.T)
-        full = jnp.concatenate([vals, jnp.concatenate(sides, axis=0)[:rows]], axis=1)
-        high = full.astype(jnp.bfloat16)
-        low = (full - high.astype(jnp.float32)).astype(jnp.bfloat16)
+            eh, el = (e.astype(jnp.float32) for e in split(edge))
+            block = jnp.concatenate([eh, el, eh, jnp.zeros((80, 128), jnp.float32)], axis=0)
+            sides.append(block.T.astype(jnp.bfloat16))
+        side = jnp.concatenate(sides, axis=0)[:rows]
         dot = functools.partial(jnp.dot, preferred_element_type=jnp.float32)
-        whi = whi_ref[...]
-        got = dot(high, whi) + (dot(low, whi) + dot(high, wlo_ref[...]))
+        got = dot(jnp.concatenate([high, low], axis=1), inner_ref[...])
+        got = got + dot(jnp.concatenate([high, side], axis=1), outer_ref[...])
         a = got[:, :bz].reshape(bx, ny, bz)
         s_ref[pl.ds(sx * bx, bx)] += got[:, bz:].reshape(bx, ny, bz)
         c_ref[pl.ds(sx * bx + R, bx)] += (-METRIC[0][2]) * a
@@ -283,14 +305,14 @@
     near = list(range(gy // 2 - 1, -1, -1))
     others = list(range(1, gx // 2))
 
-    own_pot.start()
+    own_pot.wait()
     for d in masks:
-        send_pot(pot, cx, cy, (cx, across(d)))
+        send_pot(pin.at[cx, cy], cx, cy, (cx, across(d)))
     for x in mates:
-        send_pot(pot, cx, cy, (x, cy))
-    own_band.start()
+        send_pot(pin.at[cx, cy], cx, cy, (x, cy))
     send_band(0, partner, cy)
     send_group(0, [0], far)
+    z_matrices(bz, inner_ref, outer_ref)
     reached = [0]
     for d in masks:
         wait_pot(cx, across(d))
@@ -332,7 +354,6 @@
             if k:
                 forward(x, hop)
             arrive(x, hop)
-    own_pot.wait()
     sharing = share_pot()
     send_group(1, [0] + others, near + far)
     first_edges = []
@@ -340,13 +361,14 @@
         wait_block(block[t], t == 0)
         assemble(block[t])
         first_edges.append(send_edges(0, v0, block[t], t))
-        y_pass(v0, c0, block[t])
-        if t == gx - 1:
-            wait_all(sharing)
-            assemble_potential()
         if t >= 1:
-            wait_all(first_edges[t - 1])
-            z_pass(0, v0, c0, block[t - 1], t - 1)
+            y_pass(v0, c0, block[t - 1])
+    y_pass(v0, c0, block[gx - 1])
+    wait_all(sharing)
+    assemble_potential()
+    for t in range(gx - 1):
+        wait_all(first_edges[t])
+        z_pass(0, v0, c0, block[t], t)
     for t in range(1, gx - 2):
         first_x_pass(t)
     wait_all(first_edges[gx - 1])
@@ -378,10 +400,10 @@
             ty = across(dy)
             n = t * gy + dy
             if n == 0:
-                copy = pltpu.make_async_copy(obuf.at[sx, ty], out.at[band], lsem.at[2])
+                copy = pltpu.make_async_copy(obuf.at[sx, ty], out.at[:, band], lsem.at[2])
             else:
                 copy = pltpu.make_async_remote_copy(
-                    obuf.at[sx, ty], out.at[band], osend.at[n], orecv.at[n],
+                    obuf.at[sx, ty], out.at[:, band], osend.at[n], orecv.at[n],
                     device_id=(sx, ty, cz), device_id_type=MESH,
                 )
             copy.start()
@@ -408,19 +430,19 @@
     nx, ny = gx * bx, gy * by
     assert bands == gx * gy and gz > 1 and gx >= 4 and gx & (gx - 1) == 0
     f32 = jnp.float32
-    whi, wlo = z_matrices(bz)
     anywhere = pl.BlockSpec(memory_space=pl.ANY)
-    vmem = pl.BlockSpec(memory_space=pltpu.VMEM)
     dma = pltpu.SemaphoreType.DMA
     edge = (DEGREE, gx, 2, 8, (bx * ny + 127) // 128 * 128)
     out = pl.pallas_call(
         functools.partial(kernel, gx, gy, gz, bx, by),
-        out_shape=jax.ShapeDtypeStruct((bands, bx * by, bz), f32),
-        in_specs=[anywhere, anywhere, vmem, vmem],
+        out_shape=jax.ShapeDtypeStruct((bx * by, bands, bz), f32),
+        in_specs=[anywhere] * 2,
         out_specs=anywhere,
         scratch_shapes=[
+            pltpu.VMEM((2 * bz, 2 * bz), jnp.bfloat16),
+            pltpu.VMEM((bz + 128, 2 * bz), jnp.bfloat16),
             pltpu.VMEM((gx, gy, bx * by, bz), f32),
-            pltpu.VMEM((gx, gy, bx * by, bz), f32),
+            pltpu.VMEM((gx, gy, bx, by, bz), f32),
             pltpu.VMEM((nx, ny, bz), f32),
             pltpu.VMEM((nx + 2 * R, ny + 16, bz), f32),
             pltpu.VMEM((nx + 2 * R, ny + 16, bz), f32),
@@ -439,15 +461,13 @@
             dma((3,)),
         ],
         compiler_params=pltpu.CompilerParams(
-            collective_id=0, has_side_effects=True, vmem_limit_bytes=48 * 1024 * 1024
+            collective_id=0, has_side_effects=True, vmem_limit_bytes=VMEM_BYTES
         ),
     )(
-        orbitals.reshape(bands, bx * by, bz),
-        potential.reshape(bx * by, bz),
-        whi,
-        wlo,
+        orbitals.transpose(1, 2, 0, 3).reshape(bx * by, bands, bz),
+        potential,
     )
-    return out.reshape(bands, bx, by, bz)
+    return out.reshape(bx, by, bands, bz).transpose(2, 0, 1, 3)
 
 
 def solution(mesh):

time: 74.7 us -> 68.9 us (0.922)
  Pallas kernels: 70.5 us -> 66.8 us
  local copies, waits for them, and re-layouts: 3.98 us -> 1.91 us
    pallas_call x1, Pallas kernels: 70.5 us -> 66.8 us  [local(): pl.pallas_call(functools.partial(kernel, gx, gy, gz, bx, by), out_shape=j...]
    reshape x2 -> x0, local copies, waits for them, and re-layouts: 2.59 us -> none  [the longest x1 1.7 us: local(): orbitals.reshape(bands, bx * by, bz)]
    unnamed x4 -> x3, local copies, waits for them, and re-layouts: 0.01 us -> 1.91 us
    pallas_call x1 -> x0, local copies, waits for them, and re-layouts: 1.38 us -> none  [local(): pl.pallas_call(functools.partial(kernel, gx, gy, gz, bx, by), out_shape=j...]
where the time goes in v3:
time: 68.9 us; the launch traced here: 68.8 us
  Pallas kernels  66.8 us (97%)
  local copies, waits for them, and re-layouts  1.91 us (3%)
    pallas_call x1, Pallas kernels, local(): pl.pallas_call(functools.partial(kernel, gx, gy, gz, bx, by), out_shape=j...  66.8 us
    unnamed x3, local copies, waits for them, and re-layouts  1.91 us

profile of v3, /device:TPU:0, one launch (start us, length us, event | category | flops | bytes accessed | tf_op | source)
XLA Modules:
  0.0 68.8 jit_solution(64171751889569069)
XLA Ops:
  0.0 0.0 copy-start
  0.0 0.9 %copy-done = f32[12,12,128]{2,1,0:T(8,128)S(1)} copy-done((f32[12,12,128]{2,1,0:T(8,128)S(1)}, f32[12,12,128]{2,1,0:T(8,128)}, u32[]{:S(2)}) %copy-start) | copy-done | bytes 73752
  0.9 66.8 %shard_map.28 = f32[144,16,128]{2,1,0:T(8,128)S(1)} custom-call(f32[144,16,128]{2,1,0:T(8,128)} %bitcast.7, f32[12,12,128]{2,1,0:T(8,128)S(1)} %copy-done), custom_call_target="tpu_custom_call" | custom-call | tf_op jit(solution)/shard_map/pallas_call | solution.py:436
  67.7 1.0 %copy.4 = f32[16,12,12,128]{3,0,2,1:T(8,128)} copy(f32[16,12,12,128]{3,0,2,1:T(8,128)S(1)} %bitcast.6) | data formatting | bytes 2359296
Async XLA Ops:
  0.0 0.9 %copy-start = (f32[12,12,128]{2,1,0:T(8,128)S(1)}, f32[12,12,128]{2,1,0:T(8,128)}, u32[]{:S(2)}) copy-start(f32[12,12,128]{2,1,0:T(8,128)} %pot.1) | copy-start | bytes 221188

commit v4 on v3

--- a/solution.py
+++ b/solution.py
@@ -10,7 +10,6 @@
 from jax.sharding import PartitionSpec as P
 
 DEGREE = 2
-VMEM_BYTES = 54_300_000
 SECOND = (
     -5369.0 / 1800.0,
     12.0 / 7.0,
@@ -36,7 +35,8 @@
 
 def bands_of(offset, part):
     out = []
-    for table, sign in ((FIRST, -1.0), ([-0.5 * METRIC[2][2] * c for c in SECOND[1:]], 1.0)):
+    cross = [-METRIC[1][2] * c for c in FIRST]
+    for table, sign in ((cross, -1.0), ([-0.5 * METRIC[2][2] * c for c in SECOND[1:]], 1.0)):
         acc = jnp.zeros(offset.shape, jnp.float32)
         for k in range(1, R + 1):
             value = halves(table[k - 1])[part]
@@ -46,7 +46,7 @@
     return jnp.concatenate(out, axis=1).astype(jnp.bfloat16)
 
 
-def z_matrices(bz, inner_ref, outer_ref):
+def z_matrix(bz, w_ref):
     def index(shape, dim):
         return lax.broadcasted_iota(jnp.int32, shape, dim)
 
@@ -55,19 +55,18 @@
     e = index(edge, 0)
     beyond = jnp.where(e < 8, e - 8, e - 8 + bz) - index(edge, 1)
     high, edge_high = bands_of(offset, 0), bands_of(beyond, 0)
-    inner_ref[pl.ds(0, bz), :] = high
-    inner_ref[pl.ds(bz, bz), :] = high
-    outer_ref[pl.ds(0, bz), :] = bands_of(offset, 1)
-    outer_ref[pl.ds(bz, 16), :] = edge_high
-    outer_ref[pl.ds(bz + 16, 16), :] = edge_high
-    outer_ref[pl.ds(bz + 32, 16), :] = bands_of(beyond, 1)
-    outer_ref[pl.ds(bz + 48, 80), :] = jnp.zeros((80, 2 * bz), jnp.bfloat16)
+    parts = [high, high, bands_of(offset, 1), edge_high, edge_high, bands_of(beyond, 1)]
+    parts.append(jnp.zeros((80, 2 * bz), jnp.bfloat16))
+    at = 0
+    for part in parts:
+        w_ref[pl.ds(at, part.shape[0]), :] = part
+        at += part.shape[0]
 
 
 def kernel(
     gx, gy, gz, bx, by,
     orb, pot, out,
-    inner_ref, outer_ref, vin, pin, p_ref, v0, v1, a_ref, c0, c1, s_ref, obuf, ebuf, hbuf,
+    w_ref, vin, pin, p_ref, v0, v1, a_ref, c0, c1, s_ref, obuf, ebuf, hbuf,
     isend, irecv, psend, precv, qsend, qrecv, hsend, hrecv, osend, orecv, lsem,
 ):
     bz = orb.shape[-1]
@@ -209,6 +208,16 @@
                         -1.5 * SECOND[0] - CENTER
                     )
 
+    def edge_copies(step, t):
+        return [
+            pltpu.make_async_remote_copy(
+                ebuf.at[step, t, side], hbuf.at[step, t, 1 - side],
+                hsend.at[step, t, side], hrecv.at[step, t, 1 - side],
+                device_id=(cx, cy, z), device_id_type=MESH,
+            )
+            for side, z in ((0, zl), (1, zr))
+        ]
+
     def send_edges(step, v, sx, t):
         vals = v[pl.ds(sx * bx + R, bx), pl.ds(Y0, ny), :].reshape(rows, bz)
         if padded_rows > rows:
@@ -217,16 +226,8 @@
             turned = vals[i * 128 : (i + 1) * 128].T
             ebuf[step, t, 0, :, pl.ds(i * 128, 128)] = turned[:8]
             ebuf[step, t, 1, :, pl.ds(i * 128, 128)] = turned[bz - 8 :]
-        copies = []
-        for side, z in ((0, zl), (1, zr)):
-            copy = pltpu.make_async_remote_copy(
-                ebuf.at[step, t, side], hbuf.at[step, t, 1 - side],
-                hsend.at[step, t, side], hrecv.at[step, t, 1 - side],
-                device_id=(cx, cy, z), device_id_type=MESH,
-            )
+        for copy in edge_copies(step, t):
             copy.start()
-            copies.append(copy)
-        return copies
 
     def y_pass(v, c_ref, sx):
         @pl.loop(0, bx)
@@ -259,50 +260,62 @@
             block = jnp.concatenate([eh, el, eh, jnp.zeros((80, 128), jnp.float32)], axis=0)
             sides.append(block.T.astype(jnp.bfloat16))
         side = jnp.concatenate(sides, axis=0)[:rows]
-        dot = functools.partial(jnp.dot, preferred_element_type=jnp.float32)
-        got = dot(jnp.concatenate([high, low], axis=1), inner_ref[...])
-        got = got + dot(jnp.concatenate([high, side], axis=1), outer_ref[...])
+        got = jnp.dot(
+            jnp.concatenate([high, low, high, side], axis=1), w_ref[...],
+            preferred_element_type=jnp.float32,
+        )
         a = got[:, :bz].reshape(bx, ny, bz)
         s_ref[pl.ds(sx * bx, bx)] += got[:, bz:].reshape(bx, ny, bz)
-        c_ref[pl.ds(sx * bx + R, bx)] += (-METRIC[0][2]) * a
+        c_ref[pl.ds(sx * bx + R, bx)] += (METRIC[0][2] / METRIC[1][2]) * a
         a_ref[pl.ds(sx * bx, bx), pl.ds(Y0, ny), :] = a
         for i in range(bx):
             wrap_y(a_ref, sx * bx + i)
         wrap_x(c_ref, sx)
 
-    def x_row(v, c_ref, x):
-        total = s_ref[x] + p_ref[x] * v[x + R, pl.ds(Y0, ny), :]
-        for k in range(1, R + 1):
-            total = total + (-0.5 * METRIC[0][0] * SECOND[k]) * (
-                v[x + R + k, pl.ds(Y0, ny), :] + v[x + R - k, pl.ds(Y0, ny), :]
-            )
-            total = total + FIRST[k - 1] * (c_ref[x + R + k] - c_ref[x + R - k])
-            total = total + (-METRIC[1][2] * FIRST[k - 1]) * (
-                a_ref[x, pl.ds(Y0 + k, ny), :] - a_ref[x, pl.ds(Y0 - k, ny), :]
-            )
-        return total
+    many = 4 if bx % 4 == 0 and 4 % group == 0 else group
+    tall = math.gcd(ny, 8)
+
+    def x_rows(v, c_ref, x, y):
+        vs = [v[x + i, pl.ds(Y0 + y, tall), :] for i in range(many + 2 * R)]
+        cs = [c_ref[x + i, pl.ds(y, tall), :] for i in range(many + 2 * R)]
+        totals = []
+        for g in range(many):
+            mid = g + R
+            total = s_ref[x + g, pl.ds(y, tall), :] + p_ref[x + g, pl.ds(y, tall), :] * vs[mid]
+            for k in range(1, R + 1):
+                second = vs[mid + k] + vs[mid - k]
+                first = (cs[mid + k] - cs[mid - k]) + (
+                    a_ref[x + g, pl.ds(Y0 + y + k, tall), :]
+                    - a_ref[x + g, pl.ds(Y0 + y - k, tall), :]
+                )
+                total = total + (-0.5 * METRIC[0][0] * SECOND[k]) * second
+                total = total + FIRST[k - 1] * first
+            totals.append(total)
+        return totals
 
     def wait_all(copies):
         for copy in copies:
             copy.wait()
 
     block = [lax.rem(cx + gx + t - 2 * t * odd, gx) for t in range(gx)]
-    second_edges = {}
 
     def first_x_pass(t):
         sx = block[t]
 
-        @pl.loop(0, bx)
+        @pl.loop(0, bx // many)
         def _(i):
-            x = sx * bx + i
-            v1[x + R, pl.ds(Y0, ny), :] = (1.0 / HALF_WIDTH) * x_row(v0, c0, x)
-            wrap_y(v1, x + R)
+            x = sx * bx + i * many
+            for y in range(0, ny, tall):
+                for g, total in enumerate(x_rows(v0, c0, x, y)):
+                    v1[x + g + R, pl.ds(Y0 + y, tall), :] = (1.0 / HALF_WIDTH) * total
+            for g in range(many):
+                wrap_y(v1, x + g + R)
         wrap_x(v1, sx)
-        second_edges[t] = send_edges(1, v1, sx, t)
+        send_edges(1, v1, sx, t)
         y_pass(v1, c1, sx)
 
-    far = list(range(gy - 1, gy // 2 - 1, -1))
-    near = list(range(gy // 2 - 1, -1, -1))
+    far = list(range(gy // 2, gy))
+    near = list(range(gy // 2))
     others = list(range(1, gx // 2))
 
     own_pot.wait()
@@ -311,8 +324,8 @@
     for x in mates:
         send_pot(pin.at[cx, cy], cx, cy, (x, cy))
     send_band(0, partner, cy)
-    send_group(0, [0], far)
-    z_matrices(bz, inner_ref, outer_ref)
+    send_group(0, [0], near + far)
+    z_matrix(bz, w_ref)
     reached = [0]
     for d in masks:
         wait_pot(cx, across(d))
@@ -326,55 +339,63 @@
             hops.append((m, [o for o in reached if o]))
         reached = reached + [o ^ m for o in reached]
 
-    def forward(x, hop):
+    def forward(hop):
         m, offsets = hop
         for o in offsets:
-            send_pot(pin.at[x, across(o)], x, across(o), (cx, across(m)))
-
-    def arrive(x, hop):
+            for x in [cx] + mates:
+                send_pot(pin.at[cx, across(o)], cx, across(o), (x, across(m)))
+
+    def arrive(hop):
         m, offsets = hop
         for o in offsets:
-            wait_pot(x, across(o ^ m))
+            for x in [cx] + mates:
+                wait_pot(x, across(o ^ m))
 
     for hop in hops[:1]:
-        forward(cx, hop)
-    send_group(0, others, far + near)
+        forward(hop)
+    first_group = [len(bands_out)]
+    send_group(0, others, near + far)
+    first_group.append(len(bands_out))
+
+    def enter(t):
+        wait_block(block[t], t == 0)
+        assemble(block[t])
+        send_edges(0, v0, block[t], t)
+        y_pass(v0, c0, block[t])
+
+    def enter_chip():
+        enter(0)
+        enter(1)
+
+    pl.when(odd == 0)(enter_chip)
     for k, hop in enumerate(hops):
         if k:
-            forward(cx, hop)
-        arrive(cx, hop)
+            forward(hop)
+        arrive(hop)
     for x in mates:
         for d in masks:
             wait_pot(x, across(d))
-        for hop in hops[:1]:
-            forward(x, hop)
-    send_group(0, [0], near)
-    for k, hop in enumerate(hops):
-        for x in mates:
-            if k:
-                forward(x, hop)
-            arrive(x, hop)
     sharing = share_pot()
+    for copy in bands_out[slice(*first_group)]:
+        copy.wait_send()
+    del bands_out[slice(*first_group)]
     send_group(1, [0] + others, near + far)
-    first_edges = []
-    for t in range(gx):
-        wait_block(block[t], t == 0)
-        assemble(block[t])
-        first_edges.append(send_edges(0, v0, block[t], t))
-        if t >= 1:
-            y_pass(v0, c0, block[t - 1])
-    y_pass(v0, c0, block[gx - 1])
+    pl.when(odd == 1)(enter_chip)
+    for t in (0, 1):
+        wait_all(edge_copies(0, t))
+        z_pass(0, v0, c0, block[t], t)
+    for t in range(2, gx):
+        enter(t)
     wait_all(sharing)
     assemble_potential()
-    for t in range(gx - 1):
-        wait_all(first_edges[t])
+    for t in range(2, gx - 1):
+        wait_all(edge_copies(0, t))
         z_pass(0, v0, c0, block[t], t)
     for t in range(1, gx - 2):
         first_x_pass(t)
-    wait_all(first_edges[gx - 1])
+    wait_all(edge_copies(0, gx - 1))
     z_pass(0, v0, c0, block[gx - 1], gx - 1)
-    late = [gx - 2, gx - 1, 0]
-    for t in late:
+    for t in (gx - 2, gx - 1, 0):
         first_x_pass(t)
 
     outgoing = []
@@ -382,21 +403,23 @@
     def last_x_pass(t):
         sx = block[t]
 
-        @pl.loop(0, bx // group)
+        @pl.loop(0, bx // many)
         def _(i):
-            got = []
-            for j in range(group):
-                x = sx * bx + i * group + j
-                got.append(
-                    (2.0 / HALF_WIDTH) * x_row(v1, c1, x) - v0[x + R, pl.ds(Y0, ny), :]
-                )
-            at = pl.multiple_of(i * group * by, 8)
-            for sy in range(gy):
-                obuf[sx, sy, pl.ds(at, group * by), :] = jnp.concatenate(
-                    [g[sy * by : (sy + 1) * by] for g in got], axis=0
-                )
-
-        for dy in far_first + [0]:
+            x = sx * bx + i * many
+            at = pl.multiple_of(i * many * by, 8)
+            for y in range(0, ny, tall):
+                for g, total in enumerate(x_rows(v1, c1, x, y)):
+                    got = (2.0 / HALF_WIDTH) * total - v0[x + g + R, pl.ds(Y0 + y, tall), :]
+                    low = y
+                    while low < y + tall:
+                        sy = low // by
+                        high = min(y + tall, (sy + 1) * by)
+                        obuf[sx, sy, pl.ds(at + g * by + low - sy * by, high - low), :] = got[
+                            low - y : high - y
+                        ]
+                        low = high
+
+        for dy in range(gy):
             ty = across(dy)
             n = t * gy + dy
             if n == 0:
@@ -409,10 +432,9 @@
             copy.start()
             outgoing.append(copy)
 
-    ready = list(range(1, gx - 2)) + late
     done = []
-    for t in ready:
-        wait_all(second_edges[t])
+    for t in list(range(1, gx)) + [0]:
+        wait_all(edge_copies(1, t))
         z_pass(1, v1, c1, block[t], t)
         done.append(t)
         for u in range(gx):
@@ -439,8 +461,7 @@
         in_specs=[anywhere] * 2,
         out_specs=anywhere,
         scratch_shapes=[
-            pltpu.VMEM((2 * bz, 2 * bz), jnp.bfloat16),
-            pltpu.VMEM((bz + 128, 2 * bz), jnp.bfloat16),
+            pltpu.VMEM((3 * bz + 128, 2 * bz), jnp.bfloat16),
             pltpu.VMEM((gx, gy, bx * by, bz), f32),
             pltpu.VMEM((gx, gy, bx, by, bz), f32),
             pltpu.VMEM((nx, ny, bz), f32),
@@ -461,11 +482,13 @@
             dma((3,)),
         ],
         compiler_params=pltpu.CompilerParams(
-            collective_id=0, has_side_effects=True, vmem_limit_bytes=VMEM_BYTES
+            collective_id=0, has_side_effects=True, vmem_limit_bytes=48 * 1024 * 1024
         ),
     )(
-        orbitals.transpose(1, 2, 0, 3).reshape(bx * by, bands, bz),
-        potential,
+        pltpu.with_memory_space_constraint(
+            orbitals.transpose(1, 2, 0, 3).reshape(bx * by, bands, bz), pltpu.HBM
+        ),
+        pltpu.with_memory_space_constraint(potential, pltpu.HBM),
     )
     return out.reshape(bx, by, bands, bz).transpose(2, 0, 1, 3)
 

time: 68.9 us -> 67.1 us (0.974)
  Pallas kernels: 66.8 us -> 65.9 us
  local copies, waits for them, and re-layouts: 1.91 us -> 1.02 us
    unnamed x3 -> x1, local copies, waits for them, and re-layouts: 1.91 us -> 1.02 us
    pallas_call x1, Pallas kernels: 66.8 us -> 65.9 us  [local(): pl.pallas_call(functools.partial(kernel, gx, gy, gz, bx, by), out_shape=j...]
where the time goes in v4:
time: 67.1 us; the launch traced here: 67 us
  Pallas kernels  65.9 us (98%)
  local copies, waits for them, and re-layouts  1.02 us (2%)
    pallas_call x1, Pallas kernels, local(): pl.pallas_call(functools.partial(kernel, gx, gy, gz, bx, by), out_shape=j...  65.9 us

profile of v4, /device:TPU:0, one launch (start us, length us, event | category | flops | bytes accessed | tf_op | source)
XLA Modules:
  0.0 67.0 jit_solution(11155736707729249364)
XLA Ops:
  0.0 65.9 %shard_map.28 = f32[144,16,128]{2,1,0:T(8,128)S(1)} custom-call(f32[144,16,128]{2,1,0:T(8,128)} %bitcast.7, f32[12,12,128]{2,1,0:T(8,128)} %pot.1), custom_call_target="tpu_custom_call" | custom-call | tf_op jit(solution)/shard_map/pallas_call | solution.py:458
  66.0 1.0 %copy.4 = f32[16,12,12,128]{3,0,2,1:T(8,128)} copy(f32[16,12,12,128]{3,0,2,1:T(8,128)S(1)} %bitcast.6) | data formatting | bytes 2359296

commit v5 on v4

--- a/solution.py
+++ b/solution.py
@@ -91,9 +91,9 @@
 
     far_first = list(range(gy - 1, 0, -1))
 
-    own_pot = pltpu.make_async_copy(pot, pin.at[cx, cy], lsem.at[1])
+    own_pot = pltpu.make_async_copy(pot, pin.at[cx, cy], lsem.at[0])
     own_pot.start()
-    own_band = pltpu.make_async_copy(orb.at[:, band], vin.at[cx, cy], lsem.at[0])
+    own_band = pltpu.make_async_copy(orb.at[:, band], vin.at[band], irecv.at[cx])
     own_band.start()
     barrier = pltpu.get_barrier_semaphore()
     for dx in range(gx):
@@ -116,19 +116,18 @@
     mates = [lax.rem(cx + 2 * i, gx) for i in range(1, gx // 2)]
     pot_out = []
 
-    def send_pot(src, x, y, target):
+    def send_pot(y, target):
+        i = len(pot_out)
         copy = pltpu.make_async_remote_copy(
-            src, pin.at[x, y], psend.at[len(pot_out)], precv.at[x, y],
+            pin.at[cx, y], pin.at[cx, y], psend.at[i], precv.at[i],
             device_id=target + (cz,), device_id_type=MESH,
         )
         copy.start()
         pot_out.append(copy)
-
-    def wait_pot(x, y):
-        pltpu.make_async_remote_copy(
-            pot, pin.at[x, y], psend.at[0], precv.at[x, y],
-            device_id=(partner, cy, cz), device_id_type=MESH,
-        ).wait_recv()
+        return i
+
+    def wait_pot(i):
+        pot_out[i].wait_recv()
 
     def share_pot():
         copies = []
@@ -141,33 +140,26 @@
             copies.append(copy)
         return copies
 
-    bands_out = []
-
-    def send_band(n, tx, ty):
-        copy = pltpu.make_async_remote_copy(
-            orb.at[:, tx * gy + ty], vin.at[cx, cy], isend.at[n], irecv.at[cx, cy],
+    def meet(src, dst, send, recv):
+        return pltpu.make_async_remote_copy(
+            src, dst, send, recv, device_id=(partner, cy, cz), device_id_type=MESH
+        )
+
+    def send_band(tx, ty):
+        pltpu.make_async_remote_copy(
+            orb.at[:, tx * gy + ty], vin.at[band], isend.at[0], irecv.at[cx],
             device_id=(tx, ty, cz), device_id_type=MESH,
-        )
-        copy.start()
-        bands_out.append(copy)
+        ).start()
 
     def send_group(g, pairs, ds):
         for d in ds:
             for i in pairs:
                 if i or d:
-                    n = (g * (gx // 2) + i) * gy + d
-                    send_band(n, lax.rem(chip + 2 * i + g, gx), across(d))
-
-    def wait_block(sx, own):
-        for d in range(gy):
-            sy = across(d)
-            if own and d == 0:
-                own_band.wait()
-            else:
-                pltpu.make_async_remote_copy(
-                    orb.at[:, band], vin.at[sx, sy], isend.at[0], irecv.at[sx, sy],
-                    device_id=(partner, cy, cz), device_id_type=MESH,
-                ).wait_recv()
+                    send_band(lax.rem(chip + 2 * i + g, gx), across(d))
+
+    def wait_block(sx):
+        blocks = vin.at[pl.ds(sx * gy, gy)]
+        meet(blocks, blocks, isend.at[0], irecv.at[sx]).wait_recv()
 
     def wrap_y(ref, x):
         ref[x, pl.ds(Y0 - R, R), :] = ref[x, pl.ds(Y0 + ny - R, R), :]
@@ -185,7 +177,7 @@
     def pieces(sx, i):
         at = pl.multiple_of(i * group * by, 8)
         for sy in range(gy):
-            got = vin[sx, sy, pl.ds(at, group * by), :]
+            got = vin[sx * gy + sy, pl.ds(at, group * by), :]
             for j in range(group):
                 yield sy, j, got[j * by : (j + 1) * by]
 
@@ -208,11 +200,14 @@
                         -1.5 * SECOND[0] - CENTER
                     )
 
+    def edge_wait(step, t):
+        meet(ebuf.at[step, t], hbuf.at[step, t], hsend.at[0], hrecv.at[step, t]).wait_recv()
+
     def edge_copies(step, t):
         return [
             pltpu.make_async_remote_copy(
                 ebuf.at[step, t, side], hbuf.at[step, t, 1 - side],
-                hsend.at[step, t, side], hrecv.at[step, t, 1 - side],
+                hsend.at[0], hrecv.at[step, t],
                 device_id=(cx, cy, z), device_id_type=MESH,
             )
             for side, z in ((0, zl), (1, zr))
@@ -317,22 +312,19 @@
     far = list(range(gy // 2, gy))
     near = list(range(gy // 2))
     others = list(range(1, gx // 2))
+    cross_order = far + near[::-1]
 
     own_pot.wait()
-    for d in masks:
-        send_pot(pin.at[cx, cy], cx, cy, (cx, across(d)))
-    for x in mates:
-        send_pot(pin.at[cx, cy], cx, cy, (x, cy))
-    send_band(0, partner, cy)
+    soon = [send_pot(cy, (cx, across(d))) for d in masks]
+    soon += [send_pot(cy, (x, cy)) for x in mates]
+    send_band(partner, cy)
     send_group(0, [0], near + far)
+    send_group(0, others, cross_order)
     z_matrix(bz, w_ref)
+    for i in soon:
+        wait_pot(i)
+    later = [send_pot(across(d), (x, cy)) for x in mates for d in masks]
     reached = [0]
-    for d in masks:
-        wait_pot(cx, across(d))
-    for x in mates:
-        wait_pot(x, cy)
-        for d in masks:
-            send_pot(pin.at[cx, across(d)], cx, across(d), (x, cy))
     hops = []
     for k, m in enumerate(masks):
         if k:
@@ -341,64 +333,52 @@
 
     def forward(hop):
         m, offsets = hop
-        for o in offsets:
-            for x in [cx] + mates:
-                send_pot(pin.at[cx, across(o)], cx, across(o), (x, across(m)))
-
-    def arrive(hop):
-        m, offsets = hop
-        for o in offsets:
-            for x in [cx] + mates:
-                wait_pot(x, across(o ^ m))
-
-    for hop in hops[:1]:
-        forward(hop)
-    first_group = [len(bands_out)]
-    send_group(0, others, near + far)
-    first_group.append(len(bands_out))
+        return [
+            send_pot(across(o), (x, across(m))) for o in offsets for x in [cx] + mates
+        ]
+
+    hop = [i for h in hops[:1] for i in forward(h)]
+    send_group(1, [0], near + far)
+    send_group(1, others, cross_order)
 
     def enter(t):
-        wait_block(block[t], t == 0)
+        wait_block(block[t])
         assemble(block[t])
         send_edges(0, v0, block[t], t)
         y_pass(v0, c0, block[t])
 
     def enter_chip():
-        enter(0)
-        enter(1)
+        for t in (0, 1):
+            enter(t)
+        for t in (0, 1):
+            edge_wait(0, t)
+            z_pass(0, v0, c0, block[t], t)
 
     pl.when(odd == 0)(enter_chip)
-    for k, hop in enumerate(hops):
-        if k:
-            forward(hop)
-        arrive(hop)
-    for x in mates:
-        for d in masks:
-            wait_pot(x, across(d))
+    for i in hop:
+        wait_pot(i)
+    for h in hops[1:]:
+        for i in forward(h):
+            wait_pot(i)
+    for i in later:
+        wait_pot(i)
     sharing = share_pot()
-    for copy in bands_out[slice(*first_group)]:
-        copy.wait_send()
-    del bands_out[slice(*first_group)]
-    send_group(1, [0] + others, near + far)
     pl.when(odd == 1)(enter_chip)
-    for t in (0, 1):
-        wait_all(edge_copies(0, t))
-        z_pass(0, v0, c0, block[t], t)
     for t in range(2, gx):
         enter(t)
     wait_all(sharing)
     assemble_potential()
     for t in range(2, gx - 1):
-        wait_all(edge_copies(0, t))
+        edge_wait(0, t)
         z_pass(0, v0, c0, block[t], t)
     for t in range(1, gx - 2):
         first_x_pass(t)
-    wait_all(edge_copies(0, gx - 1))
+    edge_wait(0, gx - 1)
     z_pass(0, v0, c0, block[gx - 1], gx - 1)
     for t in (gx - 2, gx - 1, 0):
         first_x_pass(t)
 
-    outgoing = []
+    own_out = []
 
     def last_x_pass(t):
         sx = block[t]
@@ -419,31 +399,38 @@
                         ]
                         low = high
 
-        for dy in range(gy):
+        for dy in cross_order:
             ty = across(dy)
             n = t * gy + dy
             if n == 0:
-                copy = pltpu.make_async_copy(obuf.at[sx, ty], out.at[:, band], lsem.at[2])
-            else:
-                copy = pltpu.make_async_remote_copy(
-                    obuf.at[sx, ty], out.at[:, band], osend.at[n], orecv.at[n],
-                    device_id=(sx, ty, cz), device_id_type=MESH,
+                own_out.append(
+                    pltpu.make_async_copy(obuf.at[sx, ty], out.at[:, band], lsem.at[1])
                 )
+                own_out[0].start()
+                continue
+            copy = pltpu.make_async_remote_copy(
+                obuf.at[sx, ty], out.at[:, band], osend.at[0], orecv.at[0],
+                device_id=(sx, ty, cz), device_id_type=MESH,
+            )
             copy.start()
-            outgoing.append(copy)
 
     done = []
     for t in list(range(1, gx)) + [0]:
-        wait_all(edge_copies(1, t))
+        edge_wait(1, t)
         z_pass(1, v1, c1, block[t], t)
         done.append(t)
         for u in range(gx):
             near = {u, (u + 1) % gx, (u - 1) % gx}
             if near <= set(done) and t in near:
                 last_x_pass(u)
-    wait_all(outgoing)
-    for copy in bands_out + pot_out:
+    own_out[0].wait()
+    for copy in pot_out:
         copy.wait_send()
+    meet(ebuf, hbuf, hsend.at[0], hrecv.at[0, 0]).wait_send()
+    sent = vin.at[pl.ds(0, gx * gy - 1)]
+    meet(sent, sent, isend.at[0], orecv.at[0]).wait_send()
+    meet(sent, sent, osend.at[0], orecv.at[0]).wait_send()
+    meet(sent, sent, osend.at[0], orecv.at[0]).wait_recv()
 
 
 def local(sizes, orbitals, potential):
@@ -451,9 +438,12 @@
     bands, bx, by, bz = orbitals.shape
     nx, ny = gx * bx, gy * by
     assert bands == gx * gy and gz > 1 and gx >= 4 and gx & (gx - 1) == 0
+    assert gy >= 2 and gy & (gy - 1) == 0
     f32 = jnp.float32
     anywhere = pl.BlockSpec(memory_space=pl.ANY)
     dma = pltpu.SemaphoreType.DMA
+    hops, mates = gy.bit_length() - 1, gx // 2 - 1
+    pots = hops + mates + hops * mates + (1 + mates) * sum(2**k - 1 for k in range(1, hops))
     edge = (DEGREE, gx, 2, 8, (bx * ny + 127) // 128 * 128)
     out = pl.pallas_call(
         functools.partial(kernel, gx, gy, gz, bx, by),
@@ -462,7 +452,7 @@
         out_specs=anywhere,
         scratch_shapes=[
             pltpu.VMEM((3 * bz + 128, 2 * bz), jnp.bfloat16),
-            pltpu.VMEM((gx, gy, bx * by, bz), f32),
+            pltpu.VMEM((gx * gy, bx * by, bz), f32),
             pltpu.VMEM((gx, gy, bx, by, bz), f32),
             pltpu.VMEM((nx, ny, bz), f32),
             pltpu.VMEM((nx + 2 * R, ny + 16, bz), f32),
@@ -474,12 +464,12 @@
             pltpu.VMEM((gx, gy, bx * by, bz), f32),
             pltpu.VMEM(edge, f32),
             pltpu.VMEM(edge, f32),
-            dma((gx * gy,)), dma((gx, gy)),
-            dma((2 * gx * gy,)), dma((gx, gy)),
-            dma((gx,)), dma((gx,)),
-            dma((DEGREE, gx, 2)), dma((DEGREE, gx, 2)),
-            dma((gx * gy,)), dma((gx * gy,)),
-            dma((3,)),
+            dma((1,)), dma((gx,)),
+            dma((pots,)), dma((pots,)),
+            dma((gx // 2,)), dma((gx // 2,)),
+            dma((1,)), dma((DEGREE, gx)),
+            dma((1,)), dma((1,)),
+            dma((2,)),
         ],
         compiler_params=pltpu.CompilerParams(
             collective_id=0, has_side_effects=True, vmem_limit_bytes=48 * 1024 * 1024

time: 67.1 us -> 65.5 us (0.976)
  Pallas kernels: 65.9 us -> 64.4 us
    pallas_call x1, Pallas kernels: 65.9 us -> 64.4 us  [local(): pl.pallas_call(functools.partial(kernel, gx, gy, gz, bx, by), out_shape=j...]
where the time goes in v5:
time: 65.5 us; the launch traced here: 65.4 us
  Pallas kernels  64.4 us (98%)
  local copies, waits for them, and re-layouts  1.02 us (2%)
    pallas_call x1, Pallas kernels, local(): pl.pallas_call(functools.partial(kernel, gx, gy, gz, bx, by), out_shape=j...  64.4 us

profile of v5, /device:TPU:0, one launch (start us, length us, event | category | flops | bytes accessed | tf_op | source)
XLA Modules:
  0.0 65.4 jit_solution(8277541484851853556)
XLA Ops:
  0.0 64.4 %shard_map.28 = f32[144,16,128]{2,1,0:T(8,128)S(1)} custom-call(f32[144,16,128]{2,1,0:T(8,128)} %bitcast.7, f32[12,12,128]{2,1,0:T(8,128)} %pot.1), custom_call_target="tpu_custom_call" | custom-call | tf_op jit(solution)/shard_map/pallas_call | solution.py:448
  64.4 1.0 %copy.4 = f32[16,12,12,128]{3,0,2,1:T(8,128)} copy(f32[16,12,12,128]{3,0,2,1:T(8,128)S(1)} %bitcast.6) | data formatting | bytes 2359296

commit v6 on v5

--- a/solution.py
+++ b/solution.py
@@ -74,6 +74,7 @@
     group = 8 // math.gcd(by, 8)
     rows = bx * ny
     padded_rows = ebuf.shape[-1]
+    tall = math.gcd(ny, 8)
     cx, cy, cz = lax.axis_index("gx"), lax.axis_index("gy"), lax.axis_index("gz")
     band = cx * gy + cy
     zl, zr = lax.rem(cz + gz - 1, gz), lax.rem(cz + 1, gz)
@@ -95,6 +96,10 @@
     own_pot.start()
     own_band = pltpu.make_async_copy(orb.at[:, band], vin.at[band], irecv.at[cx])
     own_band.start()
+    for step in range(DEGREE):
+        for t in range(gx):
+            hbuf[step, t, 0, pl.ds(0, 8 - R), :] = jnp.zeros((8 - R, padded_rows), jnp.float32)
+            hbuf[step, t, 1, pl.ds(R, 8 - R), :] = jnp.zeros((8 - R, padded_rows), jnp.float32)
     barrier = pltpu.get_barrier_semaphore()
     for dx in range(gx):
         for dy in range(gy):
@@ -201,12 +206,14 @@
                     )
 
     def edge_wait(step, t):
-        meet(ebuf.at[step, t], hbuf.at[step, t], hsend.at[0], hrecv.at[step, t]).wait_recv()
+        edges = hbuf.at[step, t, :, pl.ds(0, R)]
+        meet(edges, edges, hsend.at[0], hrecv.at[step, t]).wait_recv()
 
     def edge_copies(step, t):
         return [
             pltpu.make_async_remote_copy(
-                ebuf.at[step, t, side], hbuf.at[step, t, 1 - side],
+                ebuf.at[step, t, side, pl.ds(2 * side, R)],
+                hbuf.at[step, t, 1 - side, pl.ds(2 * side, R)],
                 hsend.at[0], hrecv.at[step, t],
                 device_id=(cx, cy, z), device_id_type=MESH,
             )
@@ -225,19 +232,21 @@
             copy.start()
 
     def y_pass(v, c_ref, sx):
-        @pl.loop(0, bx)
+        @pl.loop(0, bx // group)
         def _(i):
-            x = sx * bx + i
-            first = second = None
-            for k in range(1, R + 1):
-                up = v[x + R, pl.ds(Y0 + k, ny), :]
-                down = v[x + R, pl.ds(Y0 - k, ny), :]
-                f = (-METRIC[0][1] * FIRST[k - 1]) * (up - down)
-                s = (-0.5 * METRIC[1][1] * SECOND[k]) * (up + down)
-                first = f if first is None else first + f
-                second = s if second is None else second + s
-            c_ref[x + R] = first
-            s_ref[x] = second
+            for j in range(group):
+                x = sx * bx + i * group + j
+                for y in range(0, ny, tall):
+                    first = second = None
+                    for k in range(1, R + 1):
+                        up = v[x + R, pl.ds(Y0 + y + k, tall), :]
+                        down = v[x + R, pl.ds(Y0 + y - k, tall), :]
+                        f = (-METRIC[0][1] * FIRST[k - 1]) * (up - down)
+                        s = (-0.5 * METRIC[1][1] * SECOND[k]) * (up + down)
+                        first = f if first is None else first + f
+                        second = s if second is None else second + s
+                    c_ref[x + R, pl.ds(y, tall), :] = first
+                    s_ref[x, pl.ds(y, tall), :] = second
 
     def split(x):
         high = x.astype(jnp.bfloat16)
@@ -268,40 +277,56 @@
         wrap_x(c_ref, sx)
 
     many = 4 if bx % 4 == 0 and 4 % group == 0 else group
-    tall = math.gcd(ny, 8)
-
-    def x_rows(v, c_ref, x, y):
+
+    def along_x(v, x, y):
         vs = [v[x + i, pl.ds(Y0 + y, tall), :] for i in range(many + 2 * R)]
-        cs = [c_ref[x + i, pl.ds(y, tall), :] for i in range(many + 2 * R)]
         totals = []
         for g in range(many):
             mid = g + R
             total = s_ref[x + g, pl.ds(y, tall), :] + p_ref[x + g, pl.ds(y, tall), :] * vs[mid]
             for k in range(1, R + 1):
                 second = vs[mid + k] + vs[mid - k]
+                total = total + (-0.5 * METRIC[0][0] * SECOND[k]) * second
+            totals.append(total)
+        return totals
+
+    def crossed(c_ref, x, y, totals):
+        cs = [c_ref[x + i, pl.ds(y, tall), :] for i in range(many + 2 * R)]
+        out = []
+        for g, total in enumerate(totals):
+            mid = g + R
+            for k in range(1, R + 1):
                 first = (cs[mid + k] - cs[mid - k]) + (
                     a_ref[x + g, pl.ds(Y0 + y + k, tall), :]
                     - a_ref[x + g, pl.ds(Y0 + y - k, tall), :]
                 )
-                total = total + (-0.5 * METRIC[0][0] * SECOND[k]) * second
                 total = total + FIRST[k - 1] * first
-            totals.append(total)
-        return totals
-
-    def wait_all(copies):
-        for copy in copies:
-            copy.wait()
-
-    block = [lax.rem(cx + gx + t - 2 * t * odd, gx) for t in range(gx)]
-
-    def first_x_pass(t):
-        sx = block[t]
-
+            out.append(total)
+        return out
+
+    def before_edges(sx):
         @pl.loop(0, bx // many)
         def _(i):
             x = sx * bx + i * many
             for y in range(0, ny, tall):
-                for g, total in enumerate(x_rows(v0, c0, x, y)):
+                for g, total in enumerate(along_x(v0, x, y)):
+                    s_ref[x + g, pl.ds(y, tall), :] = total
+
+    def wait_all(copies):
+        for copy in copies:
+            copy.wait()
+
+    block = [lax.rem(cx + gx + t - 2 * t * odd, gx) for t in range(gx)]
+
+    def first_x_pass(t):
+        sx = block[t]
+
+        @pl.loop(0, bx // many)
+        def _(i):
+            x = sx * bx + i * many
+            for y in range(0, ny, tall):
+                totals = [s_ref[x + g, pl.ds(y, tall), :] for g in range(many)]
+                for g, total in enumerate(crossed(c0, x, y, totals)):
                     v1[x + g + R, pl.ds(Y0 + y, tall), :] = (1.0 / HALF_WIDTH) * total
             for g in range(many):
                 wrap_y(v1, x + g + R)
@@ -368,6 +393,8 @@
         enter(t)
     wait_all(sharing)
     assemble_potential()
+    for t in range(gx):
+        before_edges(block[t])
     for t in range(2, gx - 1):
         edge_wait(0, t)
         z_pass(0, v0, c0, block[t], t)
@@ -388,7 +415,7 @@
             x = sx * bx + i * many
             at = pl.multiple_of(i * many * by, 8)
             for y in range(0, ny, tall):
-                for g, total in enumerate(x_rows(v1, c1, x, y)):
+                for g, total in enumerate(crossed(c1, x, y, along_x(v1, x, y))):
                     got = (2.0 / HALF_WIDTH) * total - v0[x + g + R, pl.ds(Y0 + y, tall), :]
                     low = y
                     while low < y + tall:
@@ -426,7 +453,8 @@
     own_out[0].wait()
     for copy in pot_out:
         copy.wait_send()
-    meet(ebuf, hbuf, hsend.at[0], hrecv.at[0, 0]).wait_send()
+    edges = ebuf.at[:, :, :, pl.ds(0, R)]
+    meet(edges, edges, hsend.at[0], hrecv.at[0, 0]).wait_send()
     sent = vin.at[pl.ds(0, gx * gy - 1)]
     meet(sent, sent, isend.at[0], orecv.at[0]).wait_send()
     meet(sent, sent, osend.at[0], orecv.at[0]).wait_send()

time: 65.5 us -> 64.7 us (0.988)
  Pallas kernels: 64.4 us -> 63.6 us
    pallas_call x1, Pallas kernels: 64.4 us -> 63.6 us  [local(): pl.pallas_call(functools.partial(kernel, gx, gy, gz, bx, by), out_shape=j...]
where the time goes in v6:
time: 64.7 us; the launch traced here: 64.6 us
  Pallas kernels  63.6 us (98%)
  local copies, waits for them, and re-layouts  1.02 us (2%)
    pallas_call x1, Pallas kernels, local(): pl.pallas_call(functools.partial(kernel, gx, gy, gz, bx, by), out_shape=j...  63.6 us

profile of v6, /device:TPU:0, one launch (start us, length us, event | category | flops | bytes accessed | tf_op | source)
XLA Modules:
  0.0 64.6 jit_solution(15062643767607928823)
XLA Ops:
  0.0 63.6 %shard_map.28 = f32[144,16,128]{2,1,0:T(8,128)S(1)} custom-call(f32[144,16,128]{2,1,0:T(8,128)} %bitcast.7, f32[12,12,128]{2,1,0:T(8,128)} %pot.1), custom_call_target="tpu_custom_call" | custom-call | tf_op jit(solution)/shard_map/pallas_call | solution.py:476
  63.6 1.0 %copy.4 = f32[16,12,12,128]{3,0,2,1:T(8,128)} copy(f32[16,12,12,128]{3,0,2,1:T(8,128)S(1)} %bitcast.6) | data formatting | bytes 2359296

commit v7 on v6

--- a/solution.py
+++ b/solution.py
@@ -343,8 +343,8 @@
     soon = [send_pot(cy, (cx, across(d))) for d in masks]
     soon += [send_pot(cy, (x, cy)) for x in mates]
     send_band(partner, cy)
-    send_group(0, [0], near + far)
-    send_group(0, others, cross_order)
+    send_group(1, [0], near + far)
+    send_group(1, others, near + far)
     z_matrix(bz, w_ref)
     for i in soon:
         wait_pot(i)
@@ -363,8 +363,8 @@
         ]
 
     hop = [i for h in hops[:1] for i in forward(h)]
-    send_group(1, [0], near + far)
-    send_group(1, others, cross_order)
+    send_group(0, [0], near + far)
+    send_group(0, others, near + far)
 
     def enter(t):
         wait_block(block[t])
@@ -379,7 +379,7 @@
             edge_wait(0, t)
             z_pass(0, v0, c0, block[t], t)
 
-    pl.when(odd == 0)(enter_chip)
+    pl.when(odd == 1)(enter_chip)
     for i in hop:
         wait_pot(i)
     for h in hops[1:]:
@@ -388,7 +388,7 @@
     for i in later:
         wait_pot(i)
     sharing = share_pot()
-    pl.when(odd == 1)(enter_chip)
+    pl.when(odd == 0)(enter_chip)
     for t in range(2, gx):
         enter(t)
     wait_all(sharing)
@@ -446,7 +446,7 @@
         edge_wait(1, t)
         z_pass(1, v1, c1, block[t], t)
         done.append(t)
-        for u in range(gx):
+        for u in list(range(2, gx)) + [0, 1]:
             near = {u, (u + 1) % gx, (u - 1) % gx}
             if near <= set(done) and t in near:
                 last_x_pass(u)

time: 64.7 us -> 62.1 us (0.960); the launches traced: 64.6 us -> 61 us
  Pallas kernels: 63.6 us -> 60 us
    pallas_call x1, Pallas kernels: 63.6 us -> 60 us  [local(): pl.pallas_call(functools.partial(kernel, gx, gy, gz, bx, by), out_shape=j...]
where the time goes in v7:
time: 62.1 us; the launch traced here: 61 us
  Pallas kernels  60 us (97%)
  local copies, waits for them, and re-layouts  1.02 us (2%)
    pallas_call x1, Pallas kernels, local(): pl.pallas_call(functools.partial(kernel, gx, gy, gz, bx, by), out_shape=j...  60 us

profile of v7, /device:TPU:0, one launch (start us, length us, event | category | flops | bytes accessed | tf_op | source)
XLA Modules:
  0.0 61.0 jit_solution(4461652736361445455)
XLA Ops:
  0.0 60.0 %shard_map.28 = f32[144,16,128]{2,1,0:T(8,128)S(1)} custom-call(f32[144,16,128]{2,1,0:T(8,128)} %bitcast.7, f32[12,12,128]{2,1,0:T(8,128)} %pot.1), custom_call_target="tpu_custom_call" | custom-call | tf_op jit(solution)/shard_map/pallas_call | solution.py:476
  60.0 1.0 %copy.4 = f32[16,12,12,128]{3,0,2,1:T(8,128)} copy(f32[16,12,12,128]{3,0,2,1:T(8,128)S(1)} %bitcast.6) | data formatting | bytes 2359296

commit v8 on v7

--- a/solution.py
+++ b/solution.py
@@ -92,7 +92,7 @@
 
     far_first = list(range(gy - 1, 0, -1))
 
-    own_pot = pltpu.make_async_copy(pot, pin.at[cx, cy], lsem.at[0])
+    own_pot = pltpu.make_async_copy(pot, pin.at[cx * gy + cy], lsem.at[0])
     own_pot.start()
     own_band = pltpu.make_async_copy(orb.at[:, band], vin.at[band], irecv.at[cx])
     own_band.start()
@@ -121,24 +121,26 @@
     mates = [lax.rem(cx + 2 * i, gx) for i in range(1, gx // 2)]
     pot_out = []
 
-    def send_pot(y, target):
-        i = len(pot_out)
+    def send_pot(stage, y, target):
         copy = pltpu.make_async_remote_copy(
-            pin.at[cx, y], pin.at[cx, y], psend.at[i], precv.at[i],
+            pin.at[cx * gy + y], pin.at[cx * gy + y], psend.at[0], precv.at[stage],
             device_id=target + (cz,), device_id_type=MESH,
         )
         copy.start()
-        pot_out.append(copy)
-        return i
-
-    def wait_pot(i):
-        pot_out[i].wait_recv()
+        pot_out.append(stage)
+
+    def pots(count):
+        return pin.at[pl.ds(0, count)]
+
+    def wait_pot(stage):
+        blocks = pots(pot_out.count(stage))
+        meet(blocks, blocks, psend.at[0], precv.at[stage]).wait_recv()
 
     def share_pot():
         copies = []
         for i, x in enumerate([cx] + mates):
             copy = pltpu.make_async_remote_copy(
-                pin.at[x], pin.at[x], qsend.at[i], qrecv.at[i],
+                pin.at[pl.ds(x * gy, gy)], pin.at[pl.ds(x * gy, gy)], qsend.at[0], qrecv.at[0],
                 device_id=(partner, cy, cz), device_id_type=MESH,
             )
             copy.start()
@@ -201,7 +203,7 @@
             @pl.loop(0, bx)
             def _(i):
                 for sy in range(gy):
-                    p_ref[sx * bx + i, pl.ds(sy * by, by), :] = pin[sx, sy, i] + (
+                    p_ref[sx * bx + i, pl.ds(sy * by, by), :] = pin[sx * gy + sy, i] + (
                         -1.5 * SECOND[0] - CENTER
                     )
 
@@ -340,15 +342,18 @@
     cross_order = far + near[::-1]
 
     own_pot.wait()
-    soon = [send_pot(cy, (cx, across(d))) for d in masks]
-    soon += [send_pot(cy, (x, cy)) for x in mates]
+    for d in masks:
+        send_pot(0, cy, (cx, across(d)))
+    for x in mates:
+        send_pot(0, cy, (x, cy))
     send_band(partner, cy)
     send_group(1, [0], near + far)
     send_group(1, others, near + far)
     z_matrix(bz, w_ref)
-    for i in soon:
-        wait_pot(i)
-    later = [send_pot(across(d), (x, cy)) for x in mates for d in masks]
+    wait_pot(0)
+    for x in mates:
+        for d in masks:
+            send_pot(1, across(d), (x, cy))
     reached = [0]
     hops = []
     for k, m in enumerate(masks):
@@ -356,13 +361,14 @@
             hops.append((m, [o for o in reached if o]))
         reached = reached + [o ^ m for o in reached]
 
-    def forward(hop):
+    def forward(stage, hop):
         m, offsets = hop
-        return [
-            send_pot(across(o), (x, across(m))) for o in offsets for x in [cx] + mates
-        ]
-
-    hop = [i for h in hops[:1] for i in forward(h)]
+        for o in offsets:
+            for x in [cx] + mates:
+                send_pot(stage, across(o), (x, across(m)))
+
+    for hop in hops[:1]:
+        forward(2, hop)
     send_group(0, [0], near + far)
     send_group(0, others, near + far)
 
@@ -380,18 +386,17 @@
             z_pass(0, v0, c0, block[t], t)
 
     pl.when(odd == 1)(enter_chip)
-    for i in hop:
-        wait_pot(i)
-    for h in hops[1:]:
-        for i in forward(h):
-            wait_pot(i)
-    for i in later:
-        wait_pot(i)
-    sharing = share_pot()
+    for k, hop in enumerate(hops):
+        if k:
+            forward(2 + k, hop)
+        wait_pot(2 + k)
+    wait_pot(1)
+    share_pot()
     pl.when(odd == 0)(enter_chip)
     for t in range(2, gx):
         enter(t)
-    wait_all(sharing)
+    share = pots(gx // 2 * gy)
+    meet(share, share, qsend.at[0], qrecv.at[0]).wait_recv()
     assemble_potential()
     for t in range(gx):
         before_edges(block[t])
@@ -451,8 +456,8 @@
             if near <= set(done) and t in near:
                 last_x_pass(u)
     own_out[0].wait()
-    for copy in pot_out:
-        copy.wait_send()
+    meet(share, share, qsend.at[0], qrecv.at[0]).wait_send()
+    meet(pots(len(pot_out)), pots(len(pot_out)), psend.at[0], qrecv.at[0]).wait_send()
     edges = ebuf.at[:, :, :, pl.ds(0, R)]
     meet(edges, edges, hsend.at[0], hrecv.at[0, 0]).wait_send()
     sent = vin.at[pl.ds(0, gx * gy - 1)]
@@ -470,8 +475,6 @@
     f32 = jnp.float32
     anywhere = pl.BlockSpec(memory_space=pl.ANY)
     dma = pltpu.SemaphoreType.DMA
-    hops, mates = gy.bit_length() - 1, gx // 2 - 1
-    pots = hops + mates + hops * mates + (1 + mates) * sum(2**k - 1 for k in range(1, hops))
     edge = (DEGREE, gx, 2, 8, (bx * ny + 127) // 128 * 128)
     out = pl.pallas_call(
         functools.partial(kernel, gx, gy, gz, bx, by),
@@ -481,7 +484,7 @@
         scratch_shapes=[
             pltpu.VMEM((3 * bz + 128, 2 * bz), jnp.bfloat16),
             pltpu.VMEM((gx * gy, bx * by, bz), f32),
-            pltpu.VMEM((gx, gy, bx, by, bz), f32),
+            pltpu.VMEM((gx * gy, bx, by, bz), f32),
             pltpu.VMEM((nx, ny, bz), f32),
             pltpu.VMEM((nx + 2 * R, ny + 16, bz), f32),
             pltpu.VMEM((nx + 2 * R, ny + 16, bz), f32),
@@ -493,8 +496,8 @@
             pltpu.VMEM(edge, f32),
             pltpu.VMEM(edge, f32),
             dma((1,)), dma((gx,)),
-            dma((pots,)), dma((pots,)),
-            dma((gx // 2,)), dma((gx // 2,)),
+            dma((1,)), dma((gy.bit_length(),)),
+            dma((1,)), dma((1,)),
             dma((1,)), dma((DEGREE, gx)),
             dma((1,)), dma((1,)),
             dma((2,)),

time: 62.1 us -> 62 us (level)
  no operation moved by 1% of the time
where the time goes in v8:
time: 62 us; the launch traced here: 60.9 us
  Pallas kernels  59.9 us (97%)
  local copies, waits for them, and re-layouts  1.02 us (2%)
    pallas_call x1, Pallas kernels, local(): pl.pallas_call(functools.partial(kernel, gx, gy, gz, bx, by), out_shape=j...  59.9 us

profile of v8, /device:TPU:0, one launch (start us, length us, event | category | flops | bytes accessed | tf_op | source)
XLA Modules:
  0.0 60.9 jit_solution(9160932174804671068)
XLA Ops:
  0.0 59.9 %shard_map.28 = f32[144,16,128]{2,1,0:T(8,128)S(1)} custom-call(f32[144,16,128]{2,1,0:T(8,128)} %bitcast.7, f32[12,12,128]{2,1,0:T(8,128)} %pot.1), custom_call_target="tpu_custom_call" | custom-call | tf_op jit(solution)/shard_map/pallas_call | solution.py:479
  59.9 1.0 %copy.4 = f32[16,12,12,128]{3,0,2,1:T(8,128)} copy(f32[16,12,12,128]{3,0,2,1:T(8,128)S(1)} %bitcast.6) | data formatting | bytes 2359296
